TPU v7x, 128 devices: a whole 4x4x4 slice. The times are simulated.
128 devices in a mesh: gx: 8 (over y_lo, x), gy: 8 (over z, core), gz: 2 (over y_hi).
Axes of the slice: x: 4, y: 4 (y_hi: 2, y_lo: 2; y = y_hi * 2 + y_lo), z: 4, core: 2. Of those that a mesh axis runs over, the one named last changes fastest.
Arguments:
- blocks: int32 [131072, 4], P(('gx', 'gy', 'gz')), may hold values from 0 to 15, as said below
- coefficients: bfloat16 [131072, 4, 128], P(('gx', 'gy', 'gz')), may hold values from -80 to 80
- residuals: float32 [131072], P(('gx', 'gy', 'gz')), may hold values from -3000 to 3000
Outputs:
- factor: float32 [8, 2, 128, 8, 2, 128], P('gx', None, None, 'gy')
- solution: float32 [16, 128], replicated
Inputs may be any that keep to these rules, and one draw needn't show every extreme that they name: Each row names 4 different blocks.
All inputs are finite; a program needn't handle non-finite values.
Results may differ from a plain program's by a relative error of at most 0.0003.
Values sent between devices are 32-bit elements; how exact they have to be, the bound alone decides.
A program may use at most 128 MiB of HBM per device.

v0:
```python
import functools

import jax
import jax.numpy as jnp
from jax import lax
from jax.experimental import pallas as pl
from jax.experimental.pallas import tpu as pltpu
from jax.sharding import PartitionSpec as P

G = 2048
BS = 128
SB = 2 * BS
SUB = 8
VMEM_LIMIT = 60 * 1024 * 1024


def mm(a, b, ca, cb, precision=lax.Precision.HIGHEST):
    return lax.dot_general(
        a, b, (((ca,), (cb,)), ((), ())), precision=precision, preferred_element_type=jnp.float32
    )


def split(x):
    high = x.astype(jnp.bfloat16)
    return high, (x - high.astype(jnp.float32)).astype(jnp.bfloat16)


def mm3(a, b, ca, cb):
    (ah, al), (bh, bl) = split(a), b if isinstance(b, tuple) else split(b)
    return mm(ah, bh, ca, cb, None) + (mm(ah, bl, ca, cb, None) + mm(al, bh, ca, cb, None))


def panel_start(nblock, k):
    return BS * (nblock * k - (k * (k - 1)) // 2)


def gram_kernel(nblock, scale, blocks_ref, coef_ref, res_ref, out_ref, design):
    slots = coef_ref.shape[0]
    rows = coef_ref.shape[1]
    chunk = 128
    nsuper = nblock // 2

    @pl.loop(0, rows // chunk)
    def _(t):
        at = pl.ds(pl.multiple_of(t * chunk, chunk), chunk)
        idx = blocks_ref[at, :]
        labels = [jnp.broadcast_to(idx[:, s : s + 1], (chunk, BS)) for s in range(slots)]
        values = [coef_ref[s, at, :].astype(jnp.float32) for s in range(slots)]
        for b in range(nblock):
            total = jnp.where(labels[0] == b, values[0], 0.0)
            for s in range(1, slots):
                total = jnp.where(labels[s] == b, values[s], total)
            design[at, b * BS : (b + 1) * BS] = total.astype(jnp.bfloat16)

    res = res_ref[...]
    high = res.astype(jnp.bfloat16)
    rest = res - high.astype(jnp.float32)
    mid = rest.astype(jnp.bfloat16)
    low = (rest - mid.astype(jnp.float32)).astype(jnp.bfloat16)
    row = lax.broadcasted_iota(jnp.int32, (16, rows), 0)
    parts = jnp.where(
        row == 0,
        high.astype(jnp.float32),
        jnp.where(
            row == 1,
            mid.astype(jnp.float32),
            jnp.where(row == 2, low.astype(jnp.float32), 0.0),
        ),
    ).astype(jnp.bfloat16)
    base = panel_start(nblock, nblock)
    out_ref[base:, :] = jnp.zeros((out_ref.shape[0] - base, BS), jnp.float32)
    for b in range(nblock):
        part = mm(parts, design[:, b * BS : (b + 1) * BS], 1, 0, None)
        out_ref[base + b : base + b + 1, :] = jnp.sum(part, axis=0, keepdims=True) * scale

    @pl.loop(0, nsuper)
    def _(jj):
        right = design[:, pl.ds(pl.multiple_of(jj * SB, SB), SB)]
        first = pl.multiple_of(panel_start(nblock, 2 * jj), BS)
        second = pl.multiple_of(panel_start(nblock, 2 * jj + 1), BS)
        block = mm(right, right, 0, 0, None) * scale
        out_ref[pl.ds(first, SB), :] = block[:, :BS]
        out_ref[pl.ds(second, BS), :] = block[BS:, BS:]

        @pl.loop(jj + 1, nsuper)
        def _(ii):
            left = design[:, pl.ds(pl.multiple_of(ii * SB, SB), SB)]
            block = mm(left, right, 0, 0, None) * scale
            down = (ii - jj) * SB
            out_ref[pl.ds(pl.multiple_of(first + down, BS), SB), :] = block[:, :BS]
            out_ref[pl.ds(pl.multiple_of(second + down - BS, BS), SB), :] = block[:, BS:]


def factor_diag(a, e):
    sub = lax.broadcasted_iota(jnp.int32, (SUB, BS), 0)
    shape = (SUB, BS)
    count = BS // SUB

    def lane(x, j):
        return jnp.broadcast_to(x[:, j : j + 1], shape)

    def sublane(x, j):
        return jnp.broadcast_to(x[j : j + 1, :], shape)

    for p in range(count):
        base = p * SUB
        block = a[base : base + SUB, :]
        eblock = e[base : base + SUB, :]
        cols = [lane(block, base + j) for j in range(SUB)]
        scales, rows, erows, upper = [], [], [], {}
        for j in range(SUB):
            inv = lax.rsqrt(sublane(cols[j], j))
            scales.append(inv)
            mult = jnp.where(sub > j, cols[j] * inv, 0.0)
            for k in range(j + 1, SUB):
                upper[j, k] = sublane(cols[k], j) * inv
                cols[k] = cols[k] - mult * upper[j, k]
            row = sublane(block, j) * inv
            erow = sublane(eblock, j) * inv
            block = jnp.where(sub == j, row, block - mult * row)
            eblock = jnp.where(sub == j, erow, eblock - mult * erow)
            rows.append(row)
            erows.append(erow)
        a[base : base + SUB, :] = block
        e[base : base + SUB, :] = eblock
        for i in range(p + 1, count):
            at = slice(i * SUB, (i + 1) * SUB)
            below = a[at, :]
            ebelow = e[at, :]
            cols = [lane(below, base + j) for j in range(SUB)]
            for j in range(SUB):
                mult = cols[j] * scales[j]
                for k in range(j + 1, SUB):
                    cols[k] = cols[k] - mult * upper[j, k]
                below = below - mult * rows[j]
                ebelow = ebelow - mult * erows[j]
            a[at, :] = below
            e[at, :] = ebelow


def factor_kernel(nblock, place_ref, packed_ref, factor_ref, z_ref, w, inverse, a, e, y, sems):
    nsuper = nblock // 2
    size = nblock * BS
    base = panel_start(nblock, nblock)
    copies = []
    for k in range(nblock):
        begin = panel_start(nblock, k)
        copies.append(
            pltpu.make_async_copy(
                packed_ref.at[begin : begin + size - k * BS, :],
                w.at[k, k * BS : size, :],
                sems.at[k],
            )
        )
    copies.append(
        pltpu.make_async_copy(packed_ref.at[base : base + nblock, :], z_ref, sems.at[nblock])
    )
    for copy in copies:
        copy.start()
    for copy in copies:
        copy.wait()
    y[...] = jnp.zeros_like(y)
    for b in range(nblock):
        y[b // 2, 0:1, (b % 2) * BS : (b % 2 + 1) * BS] = z_ref[b : b + 1, :]
    row = lax.broadcasted_iota(jnp.int32, (BS, BS), 0)
    col = lax.broadcasted_iota(jnp.int32, (BS, BS), 1)
    eye = jnp.where(row == col, 1.0, 0.0).astype(jnp.float32)

    def wide(k, start, height):
        at = pl.ds(pl.multiple_of(start, BS), height)
        return jnp.concatenate([w[2 * k, at, :], w[2 * k + 1, at, :]], axis=1)

    @pl.loop(0, nsuper)
    def _(kk):
        top = pl.ds(pl.multiple_of(kk * SB, BS), BS)
        low = pl.ds(pl.multiple_of(kk * SB + BS, BS), BS)
        k = 2 * kk
        l21 = None
        e1 = None
        for half in range(2):
            if half == 0:
                a[...] = w[k, top, :]
            else:
                l21 = mm(w[k, low, :], e1, 1, 1)
                w[k, low, :] = l21
                a[...] = w[k + 1, low, :] - mm(l21, l21, 1, 1)
            e[...] = eye
            factor_diag(a, e)
            chol = jnp.where(row <= col, a[...], 0.0).T
            if half == 0:
                w[k, top, :] = chol
                e1 = jnp.where(row >= col, e[...], 0.0)
                inverse[kk, 0:BS, 0:BS] = e1
                inverse[kk, 0:BS, BS:SB] = jnp.zeros((BS, BS), jnp.float32)
            else:
                w[k + 1, low, :] = chol
                e2 = jnp.where(row >= col, e[...], 0.0)
                inverse[kk, BS:SB, BS:SB] = e2
                inverse[kk, BS:SB, 0:BS] = -mm(e2, mm(l21, e1, 1, 0), 1, 0)
        y[kk] = mm(y[kk], inverse[kk], 1, 1)

        @pl.loop(kk + 1, nsuper)
        def _(ii):
            at = pl.ds(pl.multiple_of(ii * SB, BS), SB)
            panel = mm3(wide(kk, ii * SB, SB), inverse[kk], 1, 1)
            w[k, at, :] = panel[:, :BS]
            w[k + 1, at, :] = panel[:, BS:]

        @pl.loop(kk + 1, nsuper)
        def _(jj):
            right = split(wide(kk, jj * SB, SB))
            y[jj] = y[jj] - mm3(y[kk], right, 1, 1)

            @pl.loop(jj, nsuper)
            def _(ii):
                at = pl.ds(pl.multiple_of(ii * SB, BS), SB)
                update = mm3(wide(kk, ii * SB, SB), right, 1, 1)
                w[2 * jj, at, :] = w[2 * jj, at, :] - update[:, :BS]
                w[2 * jj + 1, at, :] = w[2 * jj + 1, at, :] - update[:, BS:]

    @pl.loop(0, nsuper)
    def _(step):
        kk = nsuper - 1 - step

        def body(ii, total):
            return total - mm3(y[ii], wide(kk, ii * SB, SB), 1, 0)

        total = lax.fori_loop(kk + 1, nsuper, body, y[kk])
        y[kk] = mm(total, inverse[kk], 1, 0)

    for b in range(nblock):
        z_ref[b : b + 1, :] = y[b // 2, 0:1, (b % 2) * BS : (b % 2 + 1) * BS]

    per_row, per_col = factor_ref.shape[0], factor_ref.shape[2] // BS
    rows_of, cols_of = nblock // per_row, nblock // per_col
    for r in range(per_row):
        for c in range(per_col):
            rb = r * rows_of + place_ref[0]
            cb = c * cols_of + place_ref[1]
            block = w[cb, pl.ds(pl.multiple_of(rb * BS, BS), BS), :]
            keep = row + rb * BS >= col + cb * BS
            factor_ref[r, :, c * BS : (c + 1) * BS] = jnp.where(keep, block, 0.0)


def exchange_kernel(nx, ny, n_gz, term_ref, out_ref, halves, stage, slots, s1, r1, s2, r2, s3, r3, s4, r4):
    n = nx * ny
    mp, mq = lax.axis_index("gx"), lax.axis_index("gy")
    me = mp * ny + mq
    g = lax.axis_index("gz")

    def remote(src, dst, send, recv, device):
        return pltpu.make_async_remote_copy(
            src_ref=src,
            dst_ref=dst,
            send_sem=send,
            recv_sem=recv,
            device_id=device,
            device_id_type=pl.DeviceIdType.MESH,
        )

    def half(c, d):
        peer = lax.rem(g + d, n_gz)
        return remote(
            term_ref.at[c, peer],
            halves.at[d - 1, c],
            s1.at[d - 1, c],
            r1.at[d - 1, c],
            {"gz": peer},
        )

    def to_row(p, q, slot):
        at, to = p * ny + q, slot * ny + q
        return remote(stage.at[at], slots.at[to], s2.at[at], r2.at[to], {"gx": p})

    def to_owner(q, slot):
        at, to = mp * ny + q, mp * ny + slot
        return remote(stage.at[at], slots.at[to], s2.at[at], r2.at[to], {"gy": q})

    def out_cols(q, owner):
        at = mp * ny + owner
        block = out_ref.at[at, g]
        return remote(block, block, s3.at[mp * ny + q], r3.at[at], {"gy": q})

    def out_rows(p, q, owner):
        at = owner * ny + q
        block = out_ref.at[at, g]
        return remote(block, block, s3.at[p * ny + q], r3.at[at], {"gx": p})

    def across(c, d, layer):
        block = out_ref.at[c, layer]
        return remote(
            block, block, s4.at[d - 1, c], r4.at[d - 1, c], {"gz": lax.rem(g + d, n_gz)}
        )

    def combine(c):
        total = term_ref[c, g]
        for d in range(1, n_gz):
            half(c, d).wait_recv()
            total = total + halves[d - 1, c]
        return total

    @pl.loop(0, n)
    def _(i):
        q = lax.rem(mq + 1 + i // nx, ny)
        p = lax.rem(mp + 1 + i % nx, nx)
        for d in range(1, n_gz):
            half(p * ny + q, d).start()

    @pl.loop(0, ny)
    def _(i):
        q = lax.rem(mq + 1 + i, ny)

        @pl.loop(0, nx - 1)
        def _(j):
            p = lax.rem(mp + 1 + j, nx)
            stage[p * ny + q] = combine(p * ny + q)
            to_row(p, q, mp).start()

    def row_sum(q):
        at = mp * ny + q
        stage[at] = combine(at)

        @pl.loop(0, nx - 1)
        def _(j):
            p = lax.rem(mp + nx - 1 - j, nx)
            to_row(p, q, p).wait_recv()
            stage[at] = stage[at] + slots[p * ny + q]

    @pl.loop(0, ny - 1)
    def _(i):
        q = lax.rem(mq + 1 + i, ny)
        row_sum(q)
        to_owner(q, mq).start()

    row_sum(mq)
    out_ref[me, g] = stage[me]

    @pl.loop(0, ny - 1)
    def _(i):
        q = lax.rem(mq + ny - 1 - i, ny)
        to_owner(q, q).wait_recv()
        out_ref[me, g] = out_ref[me, g] + slots[mp * ny + q]

    def spread(q):
        @pl.loop(0, nx - 1)
        def _(j):
            out_rows(lax.rem(mp + 1 + j, nx), q, mp).start()

        for d in range(1, n_gz):
            across(mp * ny + q, d, g).start()

    @pl.loop(0, ny - 1)
    def _(i):
        out_cols(lax.rem(mq + 1 + i, ny), mq).start()

    spread(mq)

    @pl.loop(0, ny - 1)
    def _(i):
        q = lax.rem(mq + ny - 1 - i, ny)
        out_cols(q, q).wait_recv()
        spread(q)

    @pl.loop(0, ny)
    def _(i):
        q = lax.rem(mq + ny - i, ny)

        @pl.loop(0, nx - 1)
        def _(j):
            p = lax.rem(mp + nx - 1 - j, nx)
            out_rows(p, q, p).wait_recv()
            for d in range(1, n_gz):
                across(p * ny + q, d, g).start()

    @pl.loop(0, n)
    def _(c):
        for d in range(1, n_gz):
            across(c, d, lax.rem(g + n_gz - d, n_gz)).wait_recv()
            across(c, d, g).wait_send()
            half(c, d).wait_send()

    @pl.loop(0, ny)
    def _(q):
        @pl.loop(0, nx - 1)
        def _(j):
            p = lax.rem(mp + 1 + j, nx)
            to_row(p, q, mp).wait_send()
            out_rows(p, q, mp).wait_send()

    @pl.loop(0, ny - 1)
    def _(i):
        q = lax.rem(mq + 1 + i, ny)
        to_owner(q, mq).wait_send()
        out_cols(q, mq).wait_send()


def exchange(term, row_count, col_count, n_gz):
    n = row_count * col_count
    total, width = term.shape
    part = total // (n * n_gz)
    shape = (n, n_gz, part, width)
    vmem = pl.BlockSpec(memory_space=pltpu.VMEM)
    pair = pltpu.SemaphoreType.DMA((n_gz - 1, n))
    single = pltpu.SemaphoreType.DMA((n,))
    out = pl.pallas_call(
        functools.partial(exchange_kernel, row_count, col_count, n_gz),
        out_shape=jax.ShapeDtypeStruct(shape, jnp.float32),
        in_specs=[vmem],
        out_specs=vmem,
        scratch_shapes=[
            pltpu.VMEM((n_gz - 1, n, part, width), jnp.float32),
            pltpu.VMEM((n, part, width), jnp.float32),
            pltpu.VMEM((n, part, width), jnp.float32),
            pair,
            pair,
            single,
            single,
            single,
            single,
            pair,
            pair,
        ],
        compiler_params=pltpu.CompilerParams(vmem_limit_bytes=VMEM_LIMIT, has_side_effects=True),
    )(term.reshape(shape))
    return out.reshape(total, width)


def on_device(blocks, coefficients, residuals):
    row_count = lax.axis_size("gx")
    col_count = lax.axis_size("gy")
    devices = row_count * col_count * lax.axis_size("gz")
    rows, slots, width = coefficients.shape
    scale = 1.0 / (rows * devices)
    nblock = G // width
    nsuper = nblock // 2
    used = panel_start(nblock, nblock) + nblock
    total = -(-used // (SUB * devices)) * SUB * devices
    vmem = pl.BlockSpec(memory_space=pltpu.VMEM)
    term = pl.pallas_call(
        functools.partial(gram_kernel, nblock, scale),
        out_shape=jax.ShapeDtypeStruct((total, width), jnp.float32),
        in_specs=[vmem] * 3,
        out_specs=vmem,
        scratch_shapes=[pltpu.VMEM((rows, G), jnp.bfloat16)],
        compiler_params=pltpu.CompilerParams(vmem_limit_bytes=VMEM_LIMIT),
    )(blocks, coefficients.transpose(1, 0, 2), residuals.reshape(1, rows))
    packed = exchange(term, row_count, col_count, lax.axis_size("gz"))
    place = jnp.stack([lax.axis_index("gx"), lax.axis_index("gy")]).astype(jnp.int32)
    per_row, per_col = nblock // row_count, nblock // col_count
    factor, answer = pl.pallas_call(
        functools.partial(factor_kernel, nblock),
        out_shape=(
            jax.ShapeDtypeStruct((per_row, width, per_col * width), jnp.float32),
            jax.ShapeDtypeStruct((nblock, width), jnp.float32),
        ),
        in_specs=[pl.BlockSpec(memory_space=pltpu.SMEM), pl.BlockSpec(memory_space=pl.ANY)],
        out_specs=(vmem, vmem),
        scratch_shapes=[
            pltpu.VMEM((nblock, G, width), jnp.float32),
            pltpu.VMEM((nsuper, SB, SB), jnp.float32),
            pltpu.VMEM((width, width), jnp.float32),
            pltpu.VMEM((width, width), jnp.float32),
            pltpu.VMEM((nsuper, SUB, SB), jnp.float32),
            pltpu.SemaphoreType.DMA((nblock + 1,)),
        ],
        compiler_params=pltpu.CompilerParams(vmem_limit_bytes=VMEM_LIMIT),
    )(place, packed)
    return (factor.reshape(1, per_row, width, 1, per_col, width), answer)


def solution(mesh):
    in_specs = (
        P(("gx", "gy", "gz"), None),
        P(("gx", "gy", "gz"), None, None),
        P(("gx", "gy", "gz")),
    )
    out_specs = (P("gx", None, None, "gy", None, None), P())
    return jax.shard_map(
        on_device, mesh=mesh, in_specs=in_specs, out_specs=out_specs, check_vma=False
    )
```

profile of v0, /device:TPU:0, one launch (start us, length us, event | category | flops | bytes accessed | tf_op | source)
XLA Modules:
  0.0 493.9 jit_solution(12396283249164235106)
XLA Ops:
  0.6 0.6 pad_add_fusion.place_ref
  1.2 1.8 copy.6.blocks_ref
  3.0 2.3 copy.9
  5.3 23.3 %shard_map.50 = f32[18432,128]{1,0:T(8,128)} custom-call(s32[1024,4]{1,0:T(8,128)} %copy.6.blocks_ref, bf16[4,1024,128]{2,1,0:T(8,128)(2,1)} %bitcast.11, f32[1,1024]{1,0:T(1,128)} %bitcast.13), custom_call_target="tpu_custom_call" | custom-call | tf_op jit(solution)/shard_map/pallas_call | solution.py:439
  28.6 334.0 %shard_map.51 = f32[64,2,144,128]{3,2,1,0:T(8,128)} custom-call(f32[64,2,144,128]{3,2,1,0:T(8,128)} %bitcast.10), custom_call_target="tpu_custom_call" | custom-call | tf_op jit(solution)/shard_map/pallas_call | solution.py:405
  362.7 129.4 %shard_map.52 = (f32[2,128,256]{2,1,0:T(8,128)}, f32[16,128]{1,0:T(8,128)}) custom-call(s32[2]{0:T(128)} %pad_add_fusion.place_ref, f32[18432,128]{1,0:T(8,128)} %bitcast.9), custom_call_target="tpu_custom_call" | custom-call | tf_op jit(solution)/shard_map/pallas_call | solution.py:450
  492.1 1.8 reshape.19
where the time goes:
time: 496 us; the launch traced here: 494 us
  Pallas kernels  487 us (98%)
  local copies, waits for them, and re-layouts  5.88 us (1%)
    pallas_call x1, Pallas kernels, exchange(): pl.pallas_call(functools.partial(exchange_kernel, row_count, col_count, n...  334 us
    pallas_call x1, Pallas kernels, on_device(): pl.pallas_call(functools.partial(factor_kernel, nblock), out_shape=(jax.S...  129 us
    pallas_call x1, Pallas kernels, on_device(): pl.pallas_call(functools.partial(gram_kernel, nblock, scale), out_shape=j...  23.3 us

commit v1 on v0

--- a/solution.py
+++ b/solution.py
@@ -242,187 +242,161 @@
             factor_ref[r, :, c * BS : (c + 1) * BS] = jnp.where(keep, block, 0.0)
 
 
-def exchange_kernel(nx, ny, n_gz, term_ref, out_ref, halves, stage, slots, s1, r1, s2, r2, s3, r3, s4, r4):
-    n = nx * ny
-    mp, mq = lax.axis_index("gx"), lax.axis_index("gy")
-    me = mp * ny + mq
-    g = lax.axis_index("gz")
-
-    def remote(src, dst, send, recv, device):
+UNIT = 2 * 6 * 8 * SUB
+HALVE = 3
+
+
+def exchange_kernel(chunks, term_ref, out_ref, acc, first, recv, sends, recvs):
+    gx, gy, gz = lax.axis_index("gx"), lax.axis_index("gy"), lax.axis_index("gz")
+    x, ylo = gx % 4, gx // 4
+    z, core = gy // 2, gy % 2
+
+    def flip(v):
+        return v + 1 - 2 * (v % 2)
+
+    def gray(v):
+        return (v % 2) + (v // 2) - 2 * (v % 2) * (v // 2)
+
+    y = 2 * gz + ylo
+    ynext = 4 * (1 - ylo)
+    partner = [
+        {"gx": 4 * ylo + flip(x)},
+        {"gx": ynext + x},
+        {"gy": 2 * flip(z) + core},
+        {"gx": 4 * ylo + 3 - x},
+        {"gx": ynext + x, "gz": 1 - gz},
+        {"gy": 2 * (3 - z) + core},
+    ]
+    bit = [gray(x), gray(y), gray(z), x // 2, y // 2, z // 2]
+    mate = {"gy": 2 * z + 1 - core}
+    rows = lambda at, size: pl.ds(pl.multiple_of(at, SUB), size)
+
+    def remote(src, dst, c, s, p, device):
         return pltpu.make_async_remote_copy(
             src_ref=src,
             dst_ref=dst,
-            send_sem=send,
-            recv_sem=recv,
+            send_sem=sends.at[c, s, p],
+            recv_sem=recvs.at[c, s, p],
             device_id=device,
             device_id_type=pl.DeviceIdType.MESH,
         )
 
-    def half(c, d):
-        peer = lax.rem(g + d, n_gz)
-        return remote(
-            term_ref.at[c, peer],
-            halves.at[d - 1, c],
-            s1.at[d - 1, c],
-            r1.at[d - 1, c],
-            {"gz": peer},
-        )
-
-    def to_row(p, q, slot):
-        at, to = p * ny + q, slot * ny + q
-        return remote(stage.at[at], slots.at[to], s2.at[at], r2.at[to], {"gx": p})
-
-    def to_owner(q, slot):
-        at, to = mp * ny + q, mp * ny + slot
-        return remote(stage.at[at], slots.at[to], s2.at[at], r2.at[to], {"gy": q})
-
-    def out_cols(q, owner):
-        at = mp * ny + owner
-        block = out_ref.at[at, g]
-        return remote(block, block, s3.at[mp * ny + q], r3.at[at], {"gy": q})
-
-    def out_rows(p, q, owner):
-        at = owner * ny + q
-        block = out_ref.at[at, g]
-        return remote(block, block, s3.at[p * ny + q], r3.at[at], {"gx": p})
-
-    def across(c, d, layer):
-        block = out_ref.at[c, layer]
-        return remote(
-            block, block, s4.at[d - 1, c], r4.at[d - 1, c], {"gz": lax.rem(g + d, n_gz)}
-        )
-
-    def combine(c):
-        total = term_ref[c, g]
-        for d in range(1, n_gz):
-            half(c, d).wait_recv()
-            total = total + halves[d - 1, c]
-        return total
-
-    @pl.loop(0, n)
-    def _(i):
-        q = lax.rem(mq + 1 + i // nx, ny)
-        p = lax.rem(mp + 1 + i % nx, nx)
-        for d in range(1, n_gz):
-            half(p * ny + q, d).start()
-
-    @pl.loop(0, ny)
-    def _(i):
-        q = lax.rem(mq + 1 + i, ny)
-
-        @pl.loop(0, nx - 1)
-        def _(j):
-            p = lax.rem(mp + 1 + j, nx)
-            stage[p * ny + q] = combine(p * ny + q)
-            to_row(p, q, mp).start()
-
-    def row_sum(q):
-        at = mp * ny + q
-        stage[at] = combine(at)
-
-        @pl.loop(0, nx - 1)
-        def _(j):
-            p = lax.rem(mp + nx - 1 - j, nx)
-            to_row(p, q, p).wait_recv()
-            stage[at] = stage[at] + slots[p * ny + q]
-
-    @pl.loop(0, ny - 1)
-    def _(i):
-        q = lax.rem(mq + 1 + i, ny)
-        row_sum(q)
-        to_owner(q, mq).start()
-
-    row_sum(mq)
-    out_ref[me, g] = stage[me]
-
-    @pl.loop(0, ny - 1)
-    def _(i):
-        q = lax.rem(mq + ny - 1 - i, ny)
-        to_owner(q, q).wait_recv()
-        out_ref[me, g] = out_ref[me, g] + slots[mp * ny + q]
-
-    def spread(q):
-        @pl.loop(0, nx - 1)
-        def _(j):
-            out_rows(lax.rem(mp + 1 + j, nx), q, mp).start()
-
-        for d in range(1, n_gz):
-            across(mp * ny + q, d, g).start()
-
-    @pl.loop(0, ny - 1)
-    def _(i):
-        out_cols(lax.rem(mq + 1 + i, ny), mq).start()
-
-    spread(mq)
-
-    @pl.loop(0, ny - 1)
-    def _(i):
-        q = lax.rem(mq + ny - 1 - i, ny)
-        out_cols(q, q).wait_recv()
-        spread(q)
-
-    @pl.loop(0, ny)
-    def _(i):
-        q = lax.rem(mq + ny - i, ny)
-
-        @pl.loop(0, nx - 1)
-        def _(j):
-            p = lax.rem(mp + nx - 1 - j, nx)
-            out_rows(p, q, p).wait_recv()
-            for d in range(1, n_gz):
-                across(p * ny + q, d, g).start()
-
-    @pl.loop(0, n)
-    def _(c):
-        for d in range(1, n_gz):
-            across(c, d, lax.rem(g + n_gz - d, n_gz)).wait_recv()
-            across(c, d, g).wait_send()
-            half(c, d).wait_send()
-
-    @pl.loop(0, ny)
-    def _(q):
-        @pl.loop(0, nx - 1)
-        def _(j):
-            p = lax.rem(mp + 1 + j, nx)
-            to_row(p, q, mp).wait_send()
-            out_rows(p, q, mp).wait_send()
-
-    @pl.loop(0, ny - 1)
-    def _(i):
-        q = lax.rem(mq + 1 + i, ny)
-        to_owner(q, mq).wait_send()
-        out_cols(q, mq).wait_send()
-
-
-def exchange(term, row_count, col_count, n_gz):
-    n = row_count * col_count
+    def chunk(c):
+        base, size = chunks[c]
+        half, part = size // 2, size // 12
+        pending = {}
+        where = [0] * 6
+
+        def stage(s):
+            for p in range(6):
+                local = base // 2 + p * part
+                whole = base + core * half + p * part
+                span = part >> min(s, HALVE)
+                if s == 0:
+                    other = base + (1 - core) * half + p * part
+                    copy = remote(
+                        term_ref.at[rows(other, part), :],
+                        first.at[local : local + part, :],
+                        c, 0, p, mate,
+                    )
+                    copy.start()
+                    pending[0, p] = copy
+                    continue
+                pending[s - 1, p].wait_recv()
+                if s == 1:
+                    acc[local : local + part, :] = (
+                        term_ref[rows(whole, part), :] + first[local : local + part, :]
+                    )
+                    span = part
+                elif s <= 2 * HALVE + 1:
+                    got = part >> min(s - 1, HALVE)
+                    at = rows(local + where[p], got)
+                    slot = slots[s - 1] + base // 12 // (part // got) * 6 + p * got
+                    if s - 1 > HALVE:
+                        pending[s - 1, p].wait_send()
+                    total = acc[at, :] + recv[slot : slot + got, :]
+                    if s <= 2 * HALVE:
+                        acc[at, :] = total
+                    else:
+                        out_ref[rows(whole + where[p], got), :] = total
+                    span = got
+                if s <= HALVE:
+                    g = (p + s - 1) % 6
+                    span = part >> s
+                    keep = where[p] + bit[g] * span
+                    give = where[p] + (1 - bit[g]) * span
+                    slot = slots[s] + base // 12 // (part // span) * 6 + p * span
+                    copy = remote(
+                        acc.at[rows(local + give, span), :],
+                        recv.at[slot : slot + span, :],
+                        c, s, p, partner[g],
+                    )
+                    where[p] = keep
+                elif s <= 2 * HALVE:
+                    g = (p + s - 1) % 6
+                    slot = slots[s] + base // 12 // (part // span) * 6 + p * span
+                    copy = remote(
+                        acc.at[rows(local + where[p], span), :],
+                        recv.at[slot : slot + span, :],
+                        c, s, p, partner[g],
+                    )
+                elif s <= 3 * HALVE:
+                    level = 3 * HALVE + 1 - s
+                    g = (p + level - 1) % 6
+                    span = part >> level
+                    block = out_ref.at[rows(whole + where[p], span), :]
+                    copy = remote(block, block, c, s, p, partner[g])
+                    where[p] = where[p] - bit[g] * span
+                elif s == 3 * HALVE + 1:
+                    block = out_ref.at[rows(whole, part), :]
+                    copy = remote(block, block, c, s, p, mate)
+                else:
+                    continue
+                copy.start()
+                pending[s, p] = copy
+
+        def finish():
+            for (s, p), copy in pending.items():
+                if not HALVE < s <= 2 * HALVE:
+                    copy.wait_send()
+
+        return stage, finish
+
+    slots, at = {}, 0
+    total = sum(size for _, size in chunks) // 2
+    for s in range(1, 2 * HALVE + 1):
+        slots[s] = at
+        at += total >> min(s, HALVE)
+    runs = [chunk(c) for c in range(len(chunks))]
+    last = 3 * HALVE + 2
+    for t in range(last + len(chunks)):
+        for c, (stage, _) in enumerate(runs):
+            if 0 <= t - c <= last:
+                stage(t - c)
+    for _, finish in runs:
+        finish()
+
+
+def exchange(term, chunks):
     total, width = term.shape
-    part = total // (n * n_gz)
-    shape = (n, n_gz, part, width)
+    half = total // 2
+    landing = sum(half >> min(s, HALVE) for s in range(1, 2 * HALVE + 1))
     vmem = pl.BlockSpec(memory_space=pltpu.VMEM)
-    pair = pltpu.SemaphoreType.DMA((n_gz - 1, n))
-    single = pltpu.SemaphoreType.DMA((n,))
-    out = pl.pallas_call(
-        functools.partial(exchange_kernel, row_count, col_count, n_gz),
-        out_shape=jax.ShapeDtypeStruct(shape, jnp.float32),
+    sem = pltpu.SemaphoreType.DMA((len(chunks), 3 * HALVE + 2, 6))
+    return pl.pallas_call(
+        functools.partial(exchange_kernel, chunks),
+        out_shape=jax.ShapeDtypeStruct((total, width), jnp.float32),
         in_specs=[vmem],
         out_specs=vmem,
         scratch_shapes=[
-            pltpu.VMEM((n_gz - 1, n, part, width), jnp.float32),
-            pltpu.VMEM((n, part, width), jnp.float32),
-            pltpu.VMEM((n, part, width), jnp.float32),
-            pair,
-            pair,
-            single,
-            single,
-            single,
-            single,
-            pair,
-            pair,
+            pltpu.VMEM((half, width), jnp.float32),
+            pltpu.VMEM((half, width), jnp.float32),
+            pltpu.VMEM((landing, width), jnp.float32),
+            sem,
+            sem,
         ],
         compiler_params=pltpu.CompilerParams(vmem_limit_bytes=VMEM_LIMIT, has_side_effects=True),
-    )(term.reshape(shape))
-    return out.reshape(total, width)
+    )(term)
 
 
 def on_device(blocks, coefficients, residuals):
@@ -434,7 +408,10 @@
     nblock = G // width
     nsuper = nblock // 2
     used = panel_start(nblock, nblock) + nblock
-    total = -(-used // (SUB * devices)) * SUB * devices
+    units = -(-used // UNIT)
+    counts = [units // 3 + (i < units % 3) for i in range(3)]
+    chunks = [(UNIT * sum(counts[:i]), UNIT * counts[i]) for i in range(3)]
+    total = UNIT * units
     vmem = pl.BlockSpec(memory_space=pltpu.VMEM)
     term = pl.pallas_call(
         functools.partial(gram_kernel, nblock, scale),
@@ -444,7 +421,7 @@
         scratch_shapes=[pltpu.VMEM((rows, G), jnp.bfloat16)],
         compiler_params=pltpu.CompilerParams(vmem_limit_bytes=VMEM_LIMIT),
     )(blocks, coefficients.transpose(1, 0, 2), residuals.reshape(1, rows))
-    packed = exchange(term, row_count, col_count, lax.axis_size("gz"))
+    packed = exchange(term, chunks)
     place = jnp.stack([lax.axis_index("gx"), lax.axis_index("gy")]).astype(jnp.int32)
     per_row, per_col = nblock // row_count, nblock // col_count
     factor, answer = pl.pallas_call(

time: 496 us -> 244 us (0.49)
  Pallas kernels: 487 us -> 235 us
    pallas_call x1, Pallas kernels: 334 us -> 82.5 us  [exchange(): pl.pallas_call(functools.partial(exchange_kernel, chunks), out_shape=jax....]
where the time goes in v1:
time: 244 us; the launch traced here: 242 us
  Pallas kernels  235 us (96%)
  local copies, waits for them, and re-layouts  5.87 us (2%)
    pallas_call x1, Pallas kernels, on_device(): pl.pallas_call(functools.partial(factor_kernel, nblock), out_shape=(jax.S...  129 us
    pallas_call x1, Pallas kernels, exchange(): pl.pallas_call(functools.partial(exchange_kernel, chunks), out_shape=jax....  82.5 us
    pallas_call x1, Pallas kernels, on_device(): pl.pallas_call(functools.partial(gram_kernel, nblock, scale), out_shape=j...  23.2 us

profile of v1, /device:TPU:0, one launch (start us, length us, event | category | flops | bytes accessed | tf_op | source)
XLA Modules:
  0.0 242.2 jit_solution(9997488110139610508)
XLA Ops:
  0.6 0.6 pad_add_fusion.place_ref
  1.3 1.7 copy.6.blocks_ref
  3.0 2.4 copy.9
  5.4 23.2 %shard_map.50.term_ref = f32[17664,128]{1,0:T(8,128)} custom-call(s32[1024,4]{1,0:T(8,128)} %copy.6.blocks_ref, bf16[4,1024,128]{2,1,0:T(8,128)(2,1)} %bitcast.7, f32[1,1024]{1,0:T(1,128)} %bitcast.9), custom_call_target="tpu_custom_call" | custom-call | tf_op jit(solution)/shard_map/pallas_call | solution.py:416
  28.5 82.5 %shard_map.51.packed_ref = f32[17664,128]{1,0:T(8,128)} custom-call(f32[17664,128]{1,0:T(8,128)} %shard_map.50.term_ref), custom_call_target="tpu_custom_call" | custom-call | tf_op jit(solution)/shard_map/pallas_call | solution.py:386
  111.0 129.4 %shard_map.52 = (f32[2,128,256]{2,1,0:T(8,128)}, f32[16,128]{1,0:T(8,128)}) custom-call(s32[2]{0:T(128)} %pad_add_fusion.place_ref, f32[17664,128]{1,0:T(8,128)} %shard_map.51.packed_ref), custom_call_target="tpu_custom_call" | custom-call | tf_op jit(solution)/shard_map/pallas_call | solution.py:427
  240.4 1.8 reshape.11

commit v2 on v1

--- a/solution.py
+++ b/solution.py
@@ -11,6 +11,7 @@
 BS = 128
 SB = 2 * BS
 SUB = 8
+HB = BS // 2
 VMEM_LIMIT = 60 * 1024 * 1024
 
 
@@ -19,20 +20,224 @@
         a, b, (((ca,), (cb,)), ((), ())), precision=precision, preferred_element_type=jnp.float32
     )
 
-
 def split(x):
     high = x.astype(jnp.bfloat16)
     return high, (x - high.astype(jnp.float32)).astype(jnp.bfloat16)
 
-
 def mm3(a, b, ca, cb):
-    (ah, al), (bh, bl) = split(a), b if isinstance(b, tuple) else split(b)
-    return mm(ah, bh, ca, cb, None) + (mm(ah, bl, ca, cb, None) + mm(al, bh, ca, cb, None))
-
+    ah, al = a if isinstance(a, tuple) else split(a)
+    bh, bl = b if isinstance(b, tuple) else split(b)
+    return mm(
+        jnp.concatenate([ah, ah, al], axis=ca), jnp.concatenate([bh, bl, bh], axis=cb), ca, cb, None
+    )
 
 def panel_start(nblock, k):
     return BS * (nblock * k - (k * (k - 1)) // 2)
 
+def chol_half(x, off, fill):
+    shape = (SUB, BS)
+    sub = lax.broadcasted_iota(jnp.int32, shape, 0)
+    count = len(x)
+    x = list(x)
+
+    def lane(v, j):
+        return jnp.broadcast_to(v[:, off + j : off + j + 1], shape)
+
+    def sublane(v, j):
+        return jnp.broadcast_to(v[j : j + 1, :], shape)
+
+    def lanes(v, p):
+        return [lane(v, p * SUB + j) for j in range(SUB)]
+
+    cols = lanes(x[0], 0)
+    ahead = lanes(x[1], 1)
+    below = {i: lanes(x[i], 0) for i in range(1, count)}
+    for p in range(count):
+        if p % 2 == 1:
+            fill()
+        block = x[p]
+        scales, rows, upper = [], [], {}
+        for j in range(SUB):
+            inv = lax.rsqrt(sublane(cols[j], j))
+            mult = jnp.where(sub > j, cols[j] * inv, 0.0)
+            for k in range(j + 1, SUB):
+                upper[j, k] = sublane(cols[k], j) * inv
+                cols[k] = cols[k] - mult * upper[j, k]
+            row = sublane(block, j) * inv
+            block = jnp.where(sub == j, row, block - mult * row)
+            scales.append(inv)
+            rows.append(row)
+        x[p] = block
+        fresh, reach = {}, None
+        for i in range(p + 1, count):
+            b = below[i]
+            mults = []
+            for j in range(SUB):
+                m = b[j] * scales[j]
+                mults.append(m)
+                for k in range(j + 1, SUB):
+                    b[k] = b[k] - m * upper[j, k]
+            if i == p + 1:
+                for k in range(SUB):
+                    for j in range(SUB):
+                        ahead[k] = ahead[k] - mults[j] * sublane(mults[j], k)
+            for j in range(SUB):
+                x[i] = x[i] - mults[j] * rows[j]
+            if i > p + 1:
+                fresh[i] = lanes(x[i], p + 1)
+                if i == p + 2:
+                    reach = lanes(x[i], p + 2)
+        cols, ahead, below = ahead, reach, fresh
+    return x
+
+def chol_block(t, fill=lambda: None):
+    row = lax.broadcasted_iota(jnp.int32, (BS, BS), 0)
+    col = lax.broadcasted_iota(jnp.int32, (BS, BS), 1)
+    hrow, hcol = row[:HB], col[:HB]
+
+    def rowsof(v):
+        return [v[i * SUB : (i + 1) * SUB, :] for i in range(HB // SUB)]
+
+    zero = jnp.zeros((HB, BS), jnp.float32)
+    top = t[:HB]
+    first = jnp.where(hcol < HB, top, jnp.where(hcol - HB == hrow, 1.0, 0.0))
+    xa = jnp.concatenate(chol_half(rowsof(first), 0, fill), axis=0)
+    ea = jnp.where((hcol >= HB) & (hcol - HB <= hrow), xa, 0.0)
+    ua = mm3(ea, jnp.concatenate([zero, top], axis=0), 1, 0)
+    u12 = split(jnp.where(hcol >= HB, ua, 0.0))
+    low = t[HB:] - mm3(u12, u12, 0, 0)[HB:]
+    second = jnp.where(hcol >= HB, low, jnp.where(hcol == hrow, 1.0, 0.0))
+    xb = jnp.concatenate(chol_half(rowsof(second), HB, fill), axis=0)
+    eb = jnp.where(hcol <= hrow, xb, 0.0)
+    w = mm3(u12, ea, 0, 0)[HB:]
+    e21 = mm3(eb, jnp.concatenate([w, zero], axis=0), 1, 0)
+    lowrow = jnp.where(hcol < HB, eb, -e21)
+    inverse = pltpu.roll(jnp.concatenate([ea, lowrow], axis=0), HB, 1)
+    upper = jnp.concatenate([jnp.where(hcol < HB, jnp.where(hrow <= hcol, xa, 0.0), ua),
+                             jnp.where(hcol - HB >= hrow, xb, 0.0)], axis=0)
+    return upper.T, inverse
+
+def factor_body(nblock, place_ref, packed_ref, factor_ref, z_ref, wh, wl, tiles, y, inv_h, inv_l, arrive=None):
+    nsuper = nblock // 2
+    base = panel_start(nblock, nblock)
+
+    def at(ii):
+        return pl.ds(pl.multiple_of(ii * SB, SB), SB)
+
+    def both(j, ii):
+        return wh[j, at(ii), :], wl[j, at(ii), :]
+
+    def fetch(kk):
+        first = BS * ((2 * nblock + 1) * kk - 2 * kk * kk)
+        second = first + BS * (nblock - 2 * kk) - BS
+
+        @pl.loop(kk, nsuper)
+        def _(ii):
+            for side, begin in enumerate((first, second)):
+                rows = pl.ds(pl.multiple_of(begin + (ii - kk) * SB, BS), SB)
+                tiles[kk % 2, at(ii), side * BS : (side + 1) * BS] = packed_ref[rows, :]
+
+    for b in range(nblock):
+        y[b // 2, 0:1, (b % 2) * BS : (b % 2 + 1) * BS] = packed_ref[base + b : base + b + 1, :]
+        if b % 2 == 0:
+            y[b // 2, 1:SUB, :] = jnp.zeros((SUB - 1, SB), jnp.float32)
+    row = lax.broadcasted_iota(jnp.int32, (BS, BS), 0)
+    col = lax.broadcasted_iota(jnp.int32, (BS, BS), 1)
+    zero = jnp.zeros((BS, BS), jnp.float32)
+    wh[0, 0:SB, :] = jnp.zeros((SB, SB), jnp.bfloat16)
+    wl[0, 0:SB, :] = jnp.zeros((SB, SB), jnp.bfloat16)
+    tiles[0, nsuper * SB :, :] = jnp.zeros((SB, SB), jnp.float32)
+    fetch(0)
+    fetch(1)
+
+    @pl.loop(0, nsuper)
+    def _(kk):
+        last = jnp.maximum(kk - 1, 0)
+        here, there = kk % 2, (kk + 1) % 2
+        rest = nsuper - 1 - kk
+        cursor = [kk + 1, 0]
+
+        def filler(n):
+            first = n < rest
+            ii2, j2 = cursor
+            some = (kk > 0) & (ii2 < nsuper)
+            valid = jnp.where(first, kk > 0, some)
+            j = jnp.where(valid, jnp.where(first, last, j2), 0)
+            ii = jnp.where(valid, jnp.where(first, kk + 1 + n, ii2), 0)
+            other = jnp.where(valid, jnp.where(first, kk, kk + 1), 0)
+            spot = jnp.where(valid, jnp.where(first, here, there), 0)
+            dest = jnp.where(valid, ii, nsuper)
+            moved = jnp.where(first, j2, j2 + 1)
+            done = jnp.logical_not(first) & (moved >= kk)
+            cursor[0] = jnp.where(done, ii2 + 1, ii2)
+            cursor[1] = jnp.where(done, 0, moved)
+            tiles[spot, at(dest), :] = tiles[spot, at(dest), :] - mm3(both(j, ii), both(j, other), 1, 1)
+
+        diag = tiles[here, at(kk), :]
+        steps = iter(range(16))
+
+        def fill():
+            n = next(steps, None)
+            if n is not None:
+                filler(n)
+
+        ykk = y[kk] - jnp.where(kk > 0, mm3(y[last], both(last, kk), 1, 1), 0.0)
+        la, ea = chol_block(diag[0:BS, 0:BS], fill)
+        eas = split(ea)
+        l21 = mm3(diag[BS:SB, 0:BS], eas, 1, 1)
+        l21s = split(l21)
+        lb, eb = chol_block(diag[BS:SB, BS:SB] - mm3(l21s, l21s, 1, 1), fill)
+        ec = -mm3(eb, mm3(l21s, eas, 1, 0), 1, 0)
+        inv = split(jnp.concatenate(
+            [jnp.concatenate([ea, zero], axis=1), jnp.concatenate([ec, eb], axis=1)], axis=0))
+        low = jnp.concatenate(
+            [jnp.concatenate([la, zero], axis=1), jnp.concatenate([l21, lb], axis=1)], axis=0)
+        wh[kk, at(kk), :], wl[kk, at(kk), :] = split(low)
+        inv_h[kk], inv_l[kk] = inv
+        y[kk] = mm3(ykk, inv, 1, 1)
+
+        @pl.loop(kk + 1, nsuper)
+        def _(ii):
+            y[ii] = y[ii] - jnp.where(kk > 0, mm3(y[last], both(last, ii), 1, 1), 0.0)
+            wh[kk, at(ii), :], wl[kk, at(ii), :] = split(
+                mm3(tiles[here, at(ii), :], (inv_h[kk], inv_l[kk]), 1, 1))
+
+        @pl.when(kk + 1 < nsuper)
+        def _():
+            side = both(kk, kk + 1)
+            tiles[there, at(kk + 1), :] = tiles[there, at(kk + 1), :] - mm3(side, side, 1, 1)
+
+        @pl.when(kk + 2 < nsuper)
+        def _():
+            fetch(kk + 2)
+
+    @pl.loop(0, nsuper)
+    def _(step):
+        kk = nsuper - 1 - step
+        y[kk] = mm3(y[kk], (inv_h[kk], inv_l[kk]), 1, 0)
+        x = split(y[kk])
+
+        @pl.loop(0, kk)
+        def _(j):
+            y[j] = y[j] - mm3(x, both(j, kk), 1, 0)
+
+    for b in range(nblock):
+        z_ref[b : b + 1, :] = y[b // 2, 0:1, (b % 2) * BS : (b % 2 + 1) * BS]
+
+    per_row, per_col = factor_ref.shape[0], factor_ref.shape[2] // BS
+    rows_of, cols_of = nblock // per_row, nblock // per_col
+    for r in range(per_row):
+        for c in range(per_col):
+            rb = r * rows_of + place_ref[0]
+            cb = c * cols_of + place_ref[1]
+            rows = pl.ds(pl.multiple_of(rb * BS, BS), BS)
+            wide = wh[cb // 2, rows, :].astype(jnp.float32) + wl[cb // 2, rows, :].astype(jnp.float32)
+            block = jnp.where(cb % 2 == 0, wide[:, :BS], wide[:, BS:])
+            keep = row + rb * BS >= col + cb * BS
+            factor_ref[r, :, c * BS : (c + 1) * BS] = jnp.where(keep, block, 0.0)
+
+def factor_kernel(*args):
+    factor_body(*args)
 
 def gram_kernel(nblock, scale, blocks_ref, coef_ref, res_ref, out_ref, design):
     slots = coef_ref.shape[0]
@@ -89,157 +294,6 @@
             down = (ii - jj) * SB
             out_ref[pl.ds(pl.multiple_of(first + down, BS), SB), :] = block[:, :BS]
             out_ref[pl.ds(pl.multiple_of(second + down - BS, BS), SB), :] = block[:, BS:]
-
-
-def factor_diag(a, e):
-    sub = lax.broadcasted_iota(jnp.int32, (SUB, BS), 0)
-    shape = (SUB, BS)
-    count = BS // SUB
-
-    def lane(x, j):
-        return jnp.broadcast_to(x[:, j : j + 1], shape)
-
-    def sublane(x, j):
-        return jnp.broadcast_to(x[j : j + 1, :], shape)
-
-    for p in range(count):
-        base = p * SUB
-        block = a[base : base + SUB, :]
-        eblock = e[base : base + SUB, :]
-        cols = [lane(block, base + j) for j in range(SUB)]
-        scales, rows, erows, upper = [], [], [], {}
-        for j in range(SUB):
-            inv = lax.rsqrt(sublane(cols[j], j))
-            scales.append(inv)
-            mult = jnp.where(sub > j, cols[j] * inv, 0.0)
-            for k in range(j + 1, SUB):
-                upper[j, k] = sublane(cols[k], j) * inv
-                cols[k] = cols[k] - mult * upper[j, k]
-            row = sublane(block, j) * inv
-            erow = sublane(eblock, j) * inv
-            block = jnp.where(sub == j, row, block - mult * row)
-            eblock = jnp.where(sub == j, erow, eblock - mult * erow)
-            rows.append(row)
-            erows.append(erow)
-        a[base : base + SUB, :] = block
-        e[base : base + SUB, :] = eblock
-        for i in range(p + 1, count):
-            at = slice(i * SUB, (i + 1) * SUB)
-            below = a[at, :]
-            ebelow = e[at, :]
-            cols = [lane(below, base + j) for j in range(SUB)]
-            for j in range(SUB):
-                mult = cols[j] * scales[j]
-                for k in range(j + 1, SUB):
-                    cols[k] = cols[k] - mult * upper[j, k]
-                below = below - mult * rows[j]
-                ebelow = ebelow - mult * erows[j]
-            a[at, :] = below
-            e[at, :] = ebelow
-
-
-def factor_kernel(nblock, place_ref, packed_ref, factor_ref, z_ref, w, inverse, a, e, y, sems):
-    nsuper = nblock // 2
-    size = nblock * BS
-    base = panel_start(nblock, nblock)
-    copies = []
-    for k in range(nblock):
-        begin = panel_start(nblock, k)
-        copies.append(
-            pltpu.make_async_copy(
-                packed_ref.at[begin : begin + size - k * BS, :],
-                w.at[k, k * BS : size, :],
-                sems.at[k],
-            )
-        )
-    copies.append(
-        pltpu.make_async_copy(packed_ref.at[base : base + nblock, :], z_ref, sems.at[nblock])
-    )
-    for copy in copies:
-        copy.start()
-    for copy in copies:
-        copy.wait()
-    y[...] = jnp.zeros_like(y)
-    for b in range(nblock):
-        y[b // 2, 0:1, (b % 2) * BS : (b % 2 + 1) * BS] = z_ref[b : b + 1, :]
-    row = lax.broadcasted_iota(jnp.int32, (BS, BS), 0)
-    col = lax.broadcasted_iota(jnp.int32, (BS, BS), 1)
-    eye = jnp.where(row == col, 1.0, 0.0).astype(jnp.float32)
-
-    def wide(k, start, height):
-        at = pl.ds(pl.multiple_of(start, BS), height)
-        return jnp.concatenate([w[2 * k, at, :], w[2 * k + 1, at, :]], axis=1)
-
-    @pl.loop(0, nsuper)
-    def _(kk):
-        top = pl.ds(pl.multiple_of(kk * SB, BS), BS)
-        low = pl.ds(pl.multiple_of(kk * SB + BS, BS), BS)
-        k = 2 * kk
-        l21 = None
-        e1 = None
-        for half in range(2):
-            if half == 0:
-                a[...] = w[k, top, :]
-            else:
-                l21 = mm(w[k, low, :], e1, 1, 1)
-                w[k, low, :] = l21
-                a[...] = w[k + 1, low, :] - mm(l21, l21, 1, 1)
-            e[...] = eye
-            factor_diag(a, e)
-            chol = jnp.where(row <= col, a[...], 0.0).T
-            if half == 0:
-                w[k, top, :] = chol
-                e1 = jnp.where(row >= col, e[...], 0.0)
-                inverse[kk, 0:BS, 0:BS] = e1
-                inverse[kk, 0:BS, BS:SB] = jnp.zeros((BS, BS), jnp.float32)
-            else:
-                w[k + 1, low, :] = chol
-                e2 = jnp.where(row >= col, e[...], 0.0)
-                inverse[kk, BS:SB, BS:SB] = e2
-                inverse[kk, BS:SB, 0:BS] = -mm(e2, mm(l21, e1, 1, 0), 1, 0)
-        y[kk] = mm(y[kk], inverse[kk], 1, 1)
-
-        @pl.loop(kk + 1, nsuper)
-        def _(ii):
-            at = pl.ds(pl.multiple_of(ii * SB, BS), SB)
-            panel = mm3(wide(kk, ii * SB, SB), inverse[kk], 1, 1)
-            w[k, at, :] = panel[:, :BS]
-            w[k + 1, at, :] = panel[:, BS:]
-
-        @pl.loop(kk + 1, nsuper)
-        def _(jj):
-            right = split(wide(kk, jj * SB, SB))
-            y[jj] = y[jj] - mm3(y[kk], right, 1, 1)
-
-            @pl.loop(jj, nsuper)
-            def _(ii):
-                at = pl.ds(pl.multiple_of(ii * SB, BS), SB)
-                update = mm3(wide(kk, ii * SB, SB), right, 1, 1)
-                w[2 * jj, at, :] = w[2 * jj, at, :] - update[:, :BS]
-                w[2 * jj + 1, at, :] = w[2 * jj + 1, at, :] - update[:, BS:]
-
-    @pl.loop(0, nsuper)
-    def _(step):
-        kk = nsuper - 1 - step
-
-        def body(ii, total):
-            return total - mm3(y[ii], wide(kk, ii * SB, SB), 1, 0)
-
-        total = lax.fori_loop(kk + 1, nsuper, body, y[kk])
-        y[kk] = mm(total, inverse[kk], 1, 0)
-
-    for b in range(nblock):
-        z_ref[b : b + 1, :] = y[b // 2, 0:1, (b % 2) * BS : (b % 2 + 1) * BS]
-
-    per_row, per_col = factor_ref.shape[0], factor_ref.shape[2] // BS
-    rows_of, cols_of = nblock // per_row, nblock // per_col
-    for r in range(per_row):
-        for c in range(per_col):
-            rb = r * rows_of + place_ref[0]
-            cb = c * cols_of + place_ref[1]
-            block = w[cb, pl.ds(pl.multiple_of(rb * BS, BS), BS), :]
-            keep = row + rb * BS >= col + cb * BS
-            factor_ref[r, :, c * BS : (c + 1) * BS] = jnp.where(keep, block, 0.0)
 
 
 UNIT = 2 * 6 * 8 * SUB
@@ -430,15 +484,15 @@
             jax.ShapeDtypeStruct((per_row, width, per_col * width), jnp.float32),
             jax.ShapeDtypeStruct((nblock, width), jnp.float32),
         ),
-        in_specs=[pl.BlockSpec(memory_space=pltpu.SMEM), pl.BlockSpec(memory_space=pl.ANY)],
+        in_specs=[pl.BlockSpec(memory_space=pltpu.SMEM), vmem],
         out_specs=(vmem, vmem),
         scratch_shapes=[
-            pltpu.VMEM((nblock, G, width), jnp.float32),
-            pltpu.VMEM((nsuper, SB, SB), jnp.float32),
-            pltpu.VMEM((width, width), jnp.float32),
-            pltpu.VMEM((width, width), jnp.float32),
+            pltpu.VMEM((nsuper, G, SB), jnp.bfloat16),
+            pltpu.VMEM((nsuper, G, SB), jnp.bfloat16),
+            pltpu.VMEM((2, G + SB, SB), jnp.float32),
             pltpu.VMEM((nsuper, SUB, SB), jnp.float32),
-            pltpu.SemaphoreType.DMA((nblock + 1,)),
+            pltpu.VMEM((nsuper, SB, SB), jnp.bfloat16),
+            pltpu.VMEM((nsuper, SB, SB), jnp.bfloat16),
         ],
         compiler_params=pltpu.CompilerParams(vmem_limit_bytes=VMEM_LIMIT),
     )(place, packed)

time: 244 us -> 190 us (0.78)
  Pallas kernels: 235 us -> 181 us
    pallas_call x1, Pallas kernels: 129 us -> 75.6 us  [on_device(): pl.pallas_call(functools.partial(factor_kernel, nblock), out_shape=(jax.S...]
where the time goes in v2:
time: 190 us; the launch traced here: 188 us
  Pallas kernels  181 us (95%)
  local copies, waits for them, and re-layouts  5.87 us (3%)
    pallas_call x1, Pallas kernels, exchange(): pl.pallas_call(functools.partial(exchange_kernel, chunks), out_shape=jax....  82.5 us
    pallas_call x1, Pallas kernels, on_device(): pl.pallas_call(functools.partial(factor_kernel, nblock), out_shape=(jax.S...  75.6 us
    pallas_call x1, Pallas kernels, on_device(): pl.pallas_call(functools.partial(gram_kernel, nblock, scale), out_shape=j...  23.2 us
    unnamed x2, local copies, waits for them, and re-layouts  4.09 us

profile of v2, /device:TPU:0, one launch (start us, length us, event | category | flops | bytes accessed | tf_op | source)
XLA Modules:
  0.0 188.4 jit_solution(5574823316664295173)
XLA Ops:
  0.6 0.6 pad_add_fusion.args_0_
  1.3 1.7 copy.6.blocks_ref
  3.0 2.4 %copy.9 = bf16[1024,4,128]{2,0,1:T(8,128)(2,1)} copy(bf16[1024,4,128]{2,1,0:T(4,128)(2,1)} %param.4) | data formatting | bytes 2097152 | tf_op args[1]
  5.4 23.2 %shard_map.50.term_ref = f32[17664,128]{1,0:T(8,128)} custom-call(s32[1024,4]{1,0:T(8,128)} %copy.6.blocks_ref, bf16[4,1024,128]{2,1,0:T(8,128)(2,1)} %bitcast.7, f32[1,1024]{1,0:T(1,128)} %bitcast.9), custom_call_target="tpu_custom_call" | custom-call | tf_op jit(solution)/shard_map/pallas_call | solution.py:470
  28.5 82.5 %shard_map.51.args_1_ = f32[17664,128]{1,0:T(8,128)} custom-call(f32[17664,128]{1,0:T(8,128)} %shard_map.50.term_ref), custom_call_target="tpu_custom_call" | custom-call | tf_op jit(solution)/shard_map/pallas_call | solution.py:440
  111.0 75.6 %shard_map.52 = (f32[2,128,256]{2,1,0:T(8,128)}, f32[16,128]{1,0:T(8,128)}) custom-call(s32[2]{0:T(128)} %pad_add_fusion.args_0_, f32[17664,128]{1,0:T(8,128)} %shard_map.51.args_1_), custom_call_target="tpu_custom_call" | custom-call | tf_op jit(solution)/shard_map/pallas_call | solution.py:481
  186.6 1.8 reshape.11

commit v3 on v2

--- a/solution.py
+++ b/solution.py
@@ -12,7 +12,9 @@
 SB = 2 * BS
 SUB = 8
 HB = BS // 2
-VMEM_LIMIT = 60 * 1024 * 1024
+VMEM_LIMIT = 63 * 1024 * 1024
+UNIT = 2 * 6 * 8 * SUB
+HALVE = 3
 
 
 def mm(a, b, ca, cb, precision=lax.Precision.HIGHEST):
@@ -117,71 +119,68 @@
                              jnp.where(hcol - HB >= hrow, xb, 0.0)], axis=0)
     return upper.T, inverse
 
-def factor_body(nblock, place_ref, packed_ref, factor_ref, z_ref, wh, wl, tiles, y, inv_h, inv_l, arrive=None):
+def layout(nblock):
     nsuper = nblock // 2
-    base = panel_start(nblock, nblock)
+    sizes = [BS * (2 * nblock - 4 * j - 1) for j in range(nsuper)]
+    begins, chunks, at = {}, [], 0
+    for group in ((0, nsuper - 1), (1, 2), range(3, nsuper - 1)):
+        base = at
+        for j in group:
+            begins[j] = at
+            at += sizes[j]
+        if base == 0:
+            rhs = at
+            at += nblock
+        used = at
+        at = base + -(-(at - base) // UNIT) * UNIT
+        chunks.append((base, at - base, used))
+    return begins, rhs, chunks, at
+
+
+def factor_all(nblock, begins, rhs, packed, factor_ref, z_ref, wh, wl, tiles, y, inv_h, inv_l, hooks):
+    nsuper = nblock // 2
 
     def at(ii):
         return pl.ds(pl.multiple_of(ii * SB, SB), SB)
 
+    def spot(j, ii):
+        return (j * (2 * nsuper + 1 - j)) // 2 + ii - j
+
     def both(j, ii):
-        return wh[j, at(ii), :], wl[j, at(ii), :]
+        k = spot(j, ii)
+        return wh[k], wl[k]
+
+    def keep(j, ii, value):
+        k = spot(j, ii)
+        wh[k], wl[k] = split(value)
 
     def fetch(kk):
-        first = BS * ((2 * nblock + 1) * kk - 2 * kk * kk)
+        if isinstance(kk, int):
+            first = begins[kk]
+        else:
+            first = jnp.int32(begins[0])
+            for j in range(1, nsuper):
+                first = jnp.where(kk == j, begins[j], first)
         second = first + BS * (nblock - 2 * kk) - BS
 
         @pl.loop(kk, nsuper)
         def _(ii):
             for side, begin in enumerate((first, second)):
                 rows = pl.ds(pl.multiple_of(begin + (ii - kk) * SB, BS), SB)
-                tiles[kk % 2, at(ii), side * BS : (side + 1) * BS] = packed_ref[rows, :]
-
-    for b in range(nblock):
-        y[b // 2, 0:1, (b % 2) * BS : (b % 2 + 1) * BS] = packed_ref[base + b : base + b + 1, :]
-        if b % 2 == 0:
-            y[b // 2, 1:SUB, :] = jnp.zeros((SUB - 1, SB), jnp.float32)
+                tiles[kk % 2, at(ii), side * BS : (side + 1) * BS] = packed[rows, :]
+
     row = lax.broadcasted_iota(jnp.int32, (BS, BS), 0)
     col = lax.broadcasted_iota(jnp.int32, (BS, BS), 1)
     zero = jnp.zeros((BS, BS), jnp.float32)
-    wh[0, 0:SB, :] = jnp.zeros((SB, SB), jnp.bfloat16)
-    wl[0, 0:SB, :] = jnp.zeros((SB, SB), jnp.bfloat16)
     tiles[0, nsuper * SB :, :] = jnp.zeros((SB, SB), jnp.float32)
+    for b in range(nblock):
+        y[b // 2, 0:1, (b % 2) * BS : (b % 2 + 1) * BS] = packed[rhs + b : rhs + b + 1, :]
+        if b % 2 == 0:
+            y[b // 2, 1:SUB, :] = jnp.zeros((SUB - 1, SB), jnp.float32)
     fetch(0)
-    fetch(1)
-
-    @pl.loop(0, nsuper)
-    def _(kk):
-        last = jnp.maximum(kk - 1, 0)
-        here, there = kk % 2, (kk + 1) % 2
-        rest = nsuper - 1 - kk
-        cursor = [kk + 1, 0]
-
-        def filler(n):
-            first = n < rest
-            ii2, j2 = cursor
-            some = (kk > 0) & (ii2 < nsuper)
-            valid = jnp.where(first, kk > 0, some)
-            j = jnp.where(valid, jnp.where(first, last, j2), 0)
-            ii = jnp.where(valid, jnp.where(first, kk + 1 + n, ii2), 0)
-            other = jnp.where(valid, jnp.where(first, kk, kk + 1), 0)
-            spot = jnp.where(valid, jnp.where(first, here, there), 0)
-            dest = jnp.where(valid, ii, nsuper)
-            moved = jnp.where(first, j2, j2 + 1)
-            done = jnp.logical_not(first) & (moved >= kk)
-            cursor[0] = jnp.where(done, ii2 + 1, ii2)
-            cursor[1] = jnp.where(done, 0, moved)
-            tiles[spot, at(dest), :] = tiles[spot, at(dest), :] - mm3(both(j, ii), both(j, other), 1, 1)
-
+
+    def pivot(kk, here, ykk, fill):
         diag = tiles[here, at(kk), :]
-        steps = iter(range(16))
-
-        def fill():
-            n = next(steps, None)
-            if n is not None:
-                filler(n)
-
-        ykk = y[kk] - jnp.where(kk > 0, mm3(y[last], both(last, kk), 1, 1), 0.0)
         la, ea = chol_block(diag[0:BS, 0:BS], fill)
         eas = split(ea)
         l21 = mm3(diag[BS:SB, 0:BS], eas, 1, 1)
@@ -192,20 +191,67 @@
             [jnp.concatenate([ea, zero], axis=1), jnp.concatenate([ec, eb], axis=1)], axis=0))
         low = jnp.concatenate(
             [jnp.concatenate([la, zero], axis=1), jnp.concatenate([l21, lb], axis=1)], axis=0)
-        wh[kk, at(kk), :], wl[kk, at(kk), :] = split(low)
+        keep(kk, kk, low)
         inv_h[kk], inv_l[kk] = inv
         y[kk] = mm3(ykk, inv, 1, 1)
 
+    def solve(kk, here, ii):
+        keep(kk, ii, mm3(tiles[here, at(ii), :], (inv_h[kk], inv_l[kk]), 1, 1))
+
+    def onward(kk, there):
+        side = both(kk, kk + 1)
+        tiles[there, at(kk + 1), :] = tiles[there, at(kk + 1), :] - mm3(side, side, 1, 1)
+
+    early = iter(range(2 * SUB))
+    pivot(0, 0, y[0], lambda: hooks["pivot"](next(early)))
+
+    @pl.loop(1, nsuper)
+    def _(ii):
+        solve(0, 0, ii)
+
+    hooks["solved"]()
+    fetch(1)
+    onward(0, 1)
+    fetch(2)
+
+    @pl.loop(1, nsuper)
+    def _(kk):
+        last = kk - 1
+        here, there = kk % 2, (kk + 1) % 2
+        rest = nsuper - 1 - kk
+        cursor = [kk + 1, 0]
+
+        def filler(n):
+            first = n < rest
+            ii2, j2 = cursor
+            valid = first | (ii2 < nsuper)
+            j = jnp.where(valid, jnp.where(first, last, j2), 0)
+            ii = jnp.where(valid, jnp.where(first, kk + 1 + n, ii2), 0)
+            other = jnp.where(valid, jnp.where(first, kk, kk + 1), 0)
+            side = jnp.where(valid, jnp.where(first, here, there), 0)
+            dest = jnp.where(valid, ii, nsuper)
+            moved = jnp.where(first, j2, j2 + 1)
+            done = jnp.logical_not(first) & (moved >= kk)
+            cursor[0] = jnp.where(done, ii2 + 1, ii2)
+            cursor[1] = jnp.where(done, 0, moved)
+            tiles[side, at(dest), :] = tiles[side, at(dest), :] - mm3(both(j, ii), both(j, other), 1, 1)
+
+        steps = iter(range(2 * SUB))
+        ykk = y[kk] - mm3(y[last], both(last, kk), 1, 1)
+        pivot(kk, here, ykk, lambda: filler(next(steps)))
+
         @pl.loop(kk + 1, nsuper)
         def _(ii):
-            y[ii] = y[ii] - jnp.where(kk > 0, mm3(y[last], both(last, ii), 1, 1), 0.0)
-            wh[kk, at(ii), :], wl[kk, at(ii), :] = split(
-                mm3(tiles[here, at(ii), :], (inv_h[kk], inv_l[kk]), 1, 1))
+            y[ii] = y[ii] - mm3(y[last], both(last, ii), 1, 1)
+            solve(kk, here, ii)
 
         @pl.when(kk + 1 < nsuper)
         def _():
-            side = both(kk, kk + 1)
-            tiles[there, at(kk + 1), :] = tiles[there, at(kk + 1), :] - mm3(side, side, 1, 1)
+            onward(kk, there)
+
+        @pl.when(kk == 1)
+        def _():
+            hooks["second"]()
 
         @pl.when(kk + 2 < nsuper)
         def _():
@@ -228,22 +274,20 @@
     rows_of, cols_of = nblock // per_row, nblock // per_col
     for r in range(per_row):
         for c in range(per_col):
-            rb = r * rows_of + place_ref[0]
-            cb = c * cols_of + place_ref[1]
-            rows = pl.ds(pl.multiple_of(rb * BS, BS), BS)
-            wide = wh[cb // 2, rows, :].astype(jnp.float32) + wl[cb // 2, rows, :].astype(jnp.float32)
+            rb = r * rows_of + lax.axis_index("gx")
+            cb = c * cols_of + lax.axis_index("gy")
+            k = spot(cb // 2, jnp.maximum(rb // 2, cb // 2))
+            rows = pl.ds(pl.multiple_of((rb % 2) * BS, BS), BS)
+            wide = wh[k, rows, :].astype(jnp.float32) + wl[k, rows, :].astype(jnp.float32)
             block = jnp.where(cb % 2 == 0, wide[:, :BS], wide[:, BS:])
-            keep = row + rb * BS >= col + cb * BS
-            factor_ref[r, :, c * BS : (c + 1) * BS] = jnp.where(keep, block, 0.0)
-
-def factor_kernel(*args):
-    factor_body(*args)
-
-def gram_kernel(nblock, scale, blocks_ref, coef_ref, res_ref, out_ref, design):
+            inside = row + rb * BS >= col + cb * BS
+            factor_ref[r, :, c * BS : (c + 1) * BS] = jnp.where(inside, block, 0.0)
+
+
+def make_design(nblock, blocks_ref, coef_ref, design):
     slots = coef_ref.shape[0]
     rows = coef_ref.shape[1]
     chunk = 128
-    nsuper = nblock // 2
 
     @pl.loop(0, rows // chunk)
     def _(t):
@@ -257,6 +301,9 @@
                 total = jnp.where(labels[s] == b, values[s], total)
             design[at, b * BS : (b + 1) * BS] = total.astype(jnp.bfloat16)
 
+
+def make_rhs(nblock, scale, base, res_ref, design, term):
+    rows = res_ref.shape[1]
     res = res_ref[...]
     high = res.astype(jnp.bfloat16)
     rest = res - high.astype(jnp.float32)
@@ -272,35 +319,31 @@
             jnp.where(row == 2, low.astype(jnp.float32), 0.0),
         ),
     ).astype(jnp.bfloat16)
-    base = panel_start(nblock, nblock)
-    out_ref[base:, :] = jnp.zeros((out_ref.shape[0] - base, BS), jnp.float32)
-    for b in range(nblock):
-        part = mm(parts, design[:, b * BS : (b + 1) * BS], 1, 0, None)
-        out_ref[base + b : base + b + 1, :] = jnp.sum(part, axis=0, keepdims=True) * scale
-
-    @pl.loop(0, nsuper)
-    def _(jj):
-        right = design[:, pl.ds(pl.multiple_of(jj * SB, SB), SB)]
-        first = pl.multiple_of(panel_start(nblock, 2 * jj), BS)
-        second = pl.multiple_of(panel_start(nblock, 2 * jj + 1), BS)
-        block = mm(right, right, 0, 0, None) * scale
-        out_ref[pl.ds(first, SB), :] = block[:, :BS]
-        out_ref[pl.ds(second, BS), :] = block[BS:, BS:]
-
-        @pl.loop(jj + 1, nsuper)
-        def _(ii):
-            left = design[:, pl.ds(pl.multiple_of(ii * SB, SB), SB)]
-            block = mm(left, right, 0, 0, None) * scale
-            down = (ii - jj) * SB
-            out_ref[pl.ds(pl.multiple_of(first + down, BS), SB), :] = block[:, :BS]
-            out_ref[pl.ds(pl.multiple_of(second + down - BS, BS), SB), :] = block[:, BS:]
-
-
-UNIT = 2 * 6 * 8 * SUB
-HALVE = 3
-
-
-def exchange_kernel(chunks, term_ref, out_ref, acc, first, recv, sends, recvs):
+    for b in range(nblock // 2):
+        part = mm(parts, design[:, b * SB : (b + 1) * SB], 1, 0, None)
+        total = jnp.sum(part, axis=0, keepdims=True) * scale
+        term[base + 2 * b : base + 2 * b + 1, :] = total[:, :BS]
+        term[base + 2 * b + 1 : base + 2 * b + 2, :] = total[:, BS:]
+
+
+def gram_panel(nblock, scale, jj, begin, design, term):
+    nsuper = nblock // 2
+    right = design[:, jj * SB : (jj + 1) * SB]
+    second = begin + BS * (nblock - 2 * jj)
+    block = mm(right, right, 0, 0, None) * scale
+    term[begin : begin + SB, :] = block[:, :BS]
+    term[second : second + BS, :] = block[BS:, BS:]
+
+    @pl.loop(jj + 1, nsuper)
+    def _(ii):
+        left = design[:, pl.ds(pl.multiple_of(ii * SB, SB), SB)]
+        block = mm(left, design[:, jj * SB : (jj + 1) * SB], 0, 0, None) * scale
+        down = (ii - jj) * SB
+        term[pl.ds(pl.multiple_of(begin + down, BS), SB), :] = block[:, :BS]
+        term[pl.ds(pl.multiple_of(second + down - BS, BS), SB), :] = block[:, BS:]
+
+
+def exchanger(chunks, term_ref, out_ref, acc, recv, sends, recvs):
     gx, gy, gz = lax.axis_index("gx"), lax.axis_index("gy"), lax.axis_index("gz")
     x, ylo = gx % 4, gx // 4
     z, core = gy // 2, gy % 2
@@ -336,7 +379,7 @@
         )
 
     def chunk(c):
-        base, size = chunks[c]
+        base, size, _ = chunks[c]
         half, part = size // 2, size // 12
         pending = {}
         where = [0] * 6
@@ -350,7 +393,7 @@
                     other = base + (1 - core) * half + p * part
                     copy = remote(
                         term_ref.at[rows(other, part), :],
-                        first.at[local : local + part, :],
+                        acc.at[local : local + part, :],
                         c, 0, p, mate,
                     )
                     copy.start()
@@ -359,7 +402,7 @@
                 pending[s - 1, p].wait_recv()
                 if s == 1:
                     acc[local : local + part, :] = (
-                        term_ref[rows(whole, part), :] + first[local : local + part, :]
+                        term_ref[rows(whole, part), :] + acc[local : local + part, :]
                     )
                     span = part
                 elif s <= 2 * HALVE + 1:
@@ -417,40 +460,76 @@
         return stage, finish
 
     slots, at = {}, 0
-    total = sum(size for _, size in chunks) // 2
+    total = sum(size for _, size, _ in chunks) // 2
     for s in range(1, 2 * HALVE + 1):
         slots[s] = at
         at += total >> min(s, HALVE)
     runs = [chunk(c) for c in range(len(chunks))]
-    last = 3 * HALVE + 2
-    for t in range(last + len(chunks)):
-        for c, (stage, _) in enumerate(runs):
-            if 0 <= t - c <= last:
-                stage(t - c)
-    for _, finish in runs:
+
+    def turn(t, delays):
+        for (stage, _), delay in zip(runs, delays):
+            if 0 <= t - delay <= 3 * HALVE + 2:
+                stage(t - delay)
+
+    def finish():
+        for _, close in runs:
+            close()
+
+    def greet():
+        barrier = pltpu.get_barrier_semaphore()
+        for device in partner + [mate]:
+            pl.semaphore_signal(
+                barrier, inc=1, device_id=device, device_id_type=pl.DeviceIdType.MESH
+            )
+
+    def meet():
+        pl.semaphore_wait(pltpu.get_barrier_semaphore(), len(partner) + 1)
+
+    return turn, finish, greet, meet
+
+
+DELAYS = (0, 2, 4)
+
+
+def whole_kernel(
+    nblock, scale, blocks_ref, coef_ref, res_ref, factor_ref, z_ref,
+    design, term, acc, recv, out, wh, wl, tiles, y, inv_h, inv_l, sends, recvs,
+):
+    nsuper = nblock // 2
+    begins, rhs, chunks, _ = layout(nblock)
+    turn, finish, greet, meet = exchanger(chunks, term, out, acc, recv, sends, recvs)
+    greet()
+    for base, size, used in chunks:
+        if used < base + size:
+            term[used : base + size, :] = jnp.zeros((base + size - used, BS), jnp.float32)
+
+    def gram(j):
+        gram_panel(nblock, scale, j, begins[j], design, term)
+
+    make_design(nblock, blocks_ref, coef_ref, design)
+    make_rhs(nblock, scale, rhs, res_ref, design, term)
+    gram(0)
+    gram(nsuper - 1)
+    meet()
+    work = {0: (1,), 1: (2,), 2: (3,), 3: range(4, nsuper - 1)}
+    ready = 3 * HALVE + 2
+    for t in range(ready + 1):
+        turn(t, DELAYS)
+        for j in work.get(t, ()):
+            gram(j)
+
+    def pivot_hook(n):
+        if n == 5:
+            turn(ready + 1, DELAYS)
+        if n == 11:
+            turn(ready + 2, DELAYS)
+
+    def second_hook():
+        turn(ready + 4, DELAYS)
         finish()
 
-
-def exchange(term, chunks):
-    total, width = term.shape
-    half = total // 2
-    landing = sum(half >> min(s, HALVE) for s in range(1, 2 * HALVE + 1))
-    vmem = pl.BlockSpec(memory_space=pltpu.VMEM)
-    sem = pltpu.SemaphoreType.DMA((len(chunks), 3 * HALVE + 2, 6))
-    return pl.pallas_call(
-        functools.partial(exchange_kernel, chunks),
-        out_shape=jax.ShapeDtypeStruct((total, width), jnp.float32),
-        in_specs=[vmem],
-        out_specs=vmem,
-        scratch_shapes=[
-            pltpu.VMEM((half, width), jnp.float32),
-            pltpu.VMEM((half, width), jnp.float32),
-            pltpu.VMEM((landing, width), jnp.float32),
-            sem,
-            sem,
-        ],
-        compiler_params=pltpu.CompilerParams(vmem_limit_bytes=VMEM_LIMIT, has_side_effects=True),
-    )(term)
+    hooks = {"pivot": pivot_hook, "solved": lambda: turn(ready + 3, DELAYS), "second": second_hook}
+    factor_all(nblock, begins, rhs, out, factor_ref, z_ref, wh, wl, tiles, y, inv_h, inv_l, hooks)
 
 
 def on_device(blocks, coefficients, residuals):
@@ -461,41 +540,40 @@
     scale = 1.0 / (rows * devices)
     nblock = G // width
     nsuper = nblock // 2
-    used = panel_start(nblock, nblock) + nblock
-    units = -(-used // UNIT)
-    counts = [units // 3 + (i < units % 3) for i in range(3)]
-    chunks = [(UNIT * sum(counts[:i]), UNIT * counts[i]) for i in range(3)]
-    total = UNIT * units
+    _, _, chunks, total = layout(nblock)
+    half = total // 2
+    landing = sum(half >> min(s, HALVE) for s in range(1, 2 * HALVE + 1))
+    per_row, per_col = nblock // row_count, nblock // col_count
     vmem = pl.BlockSpec(memory_space=pltpu.VMEM)
-    term = pl.pallas_call(
-        functools.partial(gram_kernel, nblock, scale),
-        out_shape=jax.ShapeDtypeStruct((total, width), jnp.float32),
-        in_specs=[vmem] * 3,
-        out_specs=vmem,
-        scratch_shapes=[pltpu.VMEM((rows, G), jnp.bfloat16)],
-        compiler_params=pltpu.CompilerParams(vmem_limit_bytes=VMEM_LIMIT),
-    )(blocks, coefficients.transpose(1, 0, 2), residuals.reshape(1, rows))
-    packed = exchange(term, chunks)
-    place = jnp.stack([lax.axis_index("gx"), lax.axis_index("gy")]).astype(jnp.int32)
-    per_row, per_col = nblock // row_count, nblock // col_count
+    sem = pltpu.SemaphoreType.DMA((len(chunks), 3 * HALVE + 2, 6))
+    count = nsuper * (nsuper + 1) // 2
     factor, answer = pl.pallas_call(
-        functools.partial(factor_kernel, nblock),
+        functools.partial(whole_kernel, nblock, scale),
         out_shape=(
             jax.ShapeDtypeStruct((per_row, width, per_col * width), jnp.float32),
             jax.ShapeDtypeStruct((nblock, width), jnp.float32),
         ),
-        in_specs=[pl.BlockSpec(memory_space=pltpu.SMEM), vmem],
+        in_specs=[vmem] * 3,
         out_specs=(vmem, vmem),
         scratch_shapes=[
-            pltpu.VMEM((nsuper, G, SB), jnp.bfloat16),
-            pltpu.VMEM((nsuper, G, SB), jnp.bfloat16),
+            pltpu.VMEM((rows, G), jnp.bfloat16),
+            pltpu.VMEM((total, width), jnp.float32),
+            pltpu.VMEM((half, width), jnp.float32),
+            pltpu.VMEM((landing, width), jnp.float32),
+            pltpu.VMEM((total, width), jnp.float32),
+            pltpu.VMEM((count, SB, SB), jnp.bfloat16),
+            pltpu.VMEM((count, SB, SB), jnp.bfloat16),
             pltpu.VMEM((2, G + SB, SB), jnp.float32),
             pltpu.VMEM((nsuper, SUB, SB), jnp.float32),
             pltpu.VMEM((nsuper, SB, SB), jnp.bfloat16),
             pltpu.VMEM((nsuper, SB, SB), jnp.bfloat16),
+            sem,
+            sem,
         ],
-        compiler_params=pltpu.CompilerParams(vmem_limit_bytes=VMEM_LIMIT),
-    )(place, packed)
+        compiler_params=pltpu.CompilerParams(
+            vmem_limit_bytes=VMEM_LIMIT, has_side_effects=True, collective_id=0
+        ),
+    )(blocks, coefficients.transpose(1, 0, 2), residuals.reshape(1, rows))
     return (factor.reshape(1, per_row, width, 1, per_col, width), answer)
 
 

time: 190 us -> 152 us (0.80)
  Pallas kernels: 181 us -> 145 us
    pallas_call x3 -> x1, Pallas kernels: 181 us -> 145 us  [on_device(): pl.pallas_call(functools.partial(whole_kernel, nblock, scale), out_shape=...]
    unnamed x2 -> x5, local copies, waits for them, and re-layouts: 4.09 us -> 4.69 us
where the time goes in v3:
time: 152 us
  Pallas kernels  145 us (95%)
  local copies, waits for them, and re-layouts  6.48 us (4%)
    pallas_call x1, Pallas kernels, on_device(): pl.pallas_call(functools.partial(whole_kernel, nblock, scale), out_shape=...  145 us
    unnamed x5, local copies, waits for them, and re-layouts  4.69 us

profile of v3, /device:TPU:0, one launch (start us, length us, event | category | flops | bytes accessed | tf_op | source)
XLA Modules:
  0.0 152.2 jit_solution(8145669405812942261)
XLA Ops:
  0.6 1.8 %copy.6.blocks_ref = s32[1024,4]{1,0:T(8,128)} copy(s32[1024,4]{0,1:T(4,128)} %param.3) | data formatting | bytes 32768 | tf_op args[0]
  2.4 2.3 %copy.9 = bf16[1024,4,128]{2,0,1:T(8,128)(2,1)} copy(bf16[1024,4,128]{2,1,0:T(4,128)(2,1)} %param.4) | data formatting | bytes 2097152 | tf_op args[1]
  4.7 145.0 %shard_map.50 = (f32[2,128,256]{2,1,0:T(8,128)}, f32[16,128]{1,0:T(8,128)}) custom-call(s32[1024,4]{1,0:T(8,128)} %copy.6.blocks_ref, bf16[4,1024,128]{2,1,0:T(8,128)(2,1)} %bitcast.5, f32[1,1024]{1,0:T(1,128)} %bitcast.7), custom_call_target="tpu_custom_call" | custom-call | tf_op jit(solution)/shard_map/pallas_call | solution.py:550
  149.8 0.0 copy-start
  149.8 1.8 %reshape.11 = f32[1,2,128,1,2,128]{5,4,2,1,3,0:T(2,128)} reshape(f32[2,128,256]{2,1,0:T(8,128)} %get-tuple-element.4) | data formatting | bytes 524288 | tf_op jit(solution)/shard_map/reshape | solution.py:577
  151.6 0.0 copy-done
  151.6 0.6 copy.11
Async XLA Ops:
  149.8 1.8 %copy-start = (f32[16,128]{1,0:T(8,128)S(1)}, f32[16,128]{1,0:T(8,128)}, u32[]{:S(2)}) copy-start(f32[16,128]{1,0:T(8,128)} %get-tuple-element.11) | copy-start | bytes 24580

commit v4 on v3

v4 whole, which is shorter than its diff:
```python
import functools

import jax
import jax.numpy as jnp
from jax import lax
from jax.experimental import pallas as pl
from jax.experimental.pallas import tpu as pltpu
from jax.sharding import PartitionSpec as P

G = 2048
BS = 128
SB = 2 * BS
SUB = 8
HB = BS // 2
VMEM_LIMIT = 63 * 1024 * 1024
UNIT = 2 * 6 * 8 * SUB
HALVE = 3
PIECES = ((2, 4), (9,), (9,))


def mm(a, b, ca, cb, precision=lax.Precision.HIGHEST):
    return lax.dot_general(
        a, b, (((ca,), (cb,)), ((), ())), precision=precision, preferred_element_type=jnp.float32
    )

def split(x):
    high = x.astype(jnp.bfloat16)
    return high, (x - high.astype(jnp.float32)).astype(jnp.bfloat16)

def mm3(a, b, ca, cb):
    ah, al = a if isinstance(a, tuple) else split(a)
    bh, bl = b if isinstance(b, tuple) else split(b)
    return mm(
        jnp.concatenate([ah, ah, al], axis=ca), jnp.concatenate([bh, bl, bh], axis=cb), ca, cb, None
    )

def panel_start(nblock, k):
    return BS * (nblock * k - (k * (k - 1)) // 2)

def chol_half(x, off, fill):
    shape = (SUB, BS)
    sub = lax.broadcasted_iota(jnp.int32, shape, 0)
    count = len(x)
    x = list(x)

    def lane(v, j):
        return jnp.broadcast_to(v[:, off + j : off + j + 1], shape)

    def sublane(v, j):
        return jnp.broadcast_to(v[j : j + 1, :], shape)

    def lanes(v, p):
        return [lane(v, p * SUB + j) for j in range(SUB)]

    cols = lanes(x[0], 0)
    ahead = lanes(x[1], 1)
    below = {i: lanes(x[i], 0) for i in range(1, count)}
    for p in range(count):
        if p % 2 == 1:
            fill()
        block = x[p]
        scales, rows, upper = [], [], {}
        for j in range(SUB):
            inv = lax.rsqrt(sublane(cols[j], j))
            mult = jnp.where(sub > j, cols[j] * inv, 0.0)
            for k in range(j + 1, SUB):
                upper[j, k] = sublane(cols[k], j) * inv
                cols[k] = cols[k] - mult * upper[j, k]
            row = sublane(block, j) * inv
            block = jnp.where(sub == j, row, block - mult * row)
            scales.append(inv)
            rows.append(row)
        x[p] = block
        fresh, reach = {}, None
        for i in range(p + 1, count):
            b = below[i]
            mults = []
            for j in range(SUB):
                m = b[j] * scales[j]
                mults.append(m)
                for k in range(j + 1, SUB):
                    b[k] = b[k] - m * upper[j, k]
            if i == p + 1:
                for k in range(SUB):
                    for j in range(SUB):
                        ahead[k] = ahead[k] - mults[j] * sublane(mults[j], k)
            for j in range(SUB):
                x[i] = x[i] - mults[j] * rows[j]
            if i > p + 1:
                fresh[i] = lanes(x[i], p + 1)
                if i == p + 2:
                    reach = lanes(x[i], p + 2)
        cols, ahead, below = ahead, reach, fresh
    return x

def chol_block(t, fill=lambda: None):
    row = lax.broadcasted_iota(jnp.int32, (BS, BS), 0)
    col = lax.broadcasted_iota(jnp.int32, (BS, BS), 1)
    hrow, hcol = row[:HB], col[:HB]

    def rowsof(v):
        return [v[i * SUB : (i + 1) * SUB, :] for i in range(HB // SUB)]

    zero = jnp.zeros((HB, BS), jnp.float32)
    top = t[:HB]
    first = jnp.where(hcol < HB, top, jnp.where(hcol - HB == hrow, 1.0, 0.0))
    xa = jnp.concatenate(chol_half(rowsof(first), 0, fill), axis=0)
    ea = jnp.where((hcol >= HB) & (hcol - HB <= hrow), xa, 0.0)
    ua = mm3(ea, jnp.concatenate([zero, top], axis=0), 1, 0)
    u12 = split(jnp.where(hcol >= HB, ua, 0.0))
    low = t[HB:] - mm3(u12, u12, 0, 0)[HB:]
    second = jnp.where(hcol >= HB, low, jnp.where(hcol == hrow, 1.0, 0.0))
    xb = jnp.concatenate(chol_half(rowsof(second), HB, fill), axis=0)
    eb = jnp.where(hcol <= hrow, xb, 0.0)
    w = mm3(u12, ea, 0, 0)[HB:]
    e21 = mm3(eb, jnp.concatenate([w, zero], axis=0), 1, 0)
    lowrow = jnp.where(hcol < HB, eb, -e21)
    inverse = pltpu.roll(jnp.concatenate([ea, lowrow], axis=0), HB, 1)
    upper = jnp.concatenate([jnp.where(hcol < HB, jnp.where(hrow <= hcol, xa, 0.0), ua),
                             jnp.where(hcol - HB >= hrow, xb, 0.0)], axis=0)
    return upper.T, inverse

def layout(nblock):
    nsuper = nblock // 2
    sizes = [BS * (2 * nblock - 4 * j - 1) for j in range(nsuper)]
    begins, chunks, pads, at = {}, [], [], 0
    for group, pieces in zip(((0, nsuper - 1), (1, 2), range(3, nsuper - 1)), PIECES):
        base = at
        for j in group:
            begins[j] = at
            at += sizes[j]
        if base == 0:
            rhs = at
            at += nblock
        pads.append((at, base + UNIT * sum(pieces)))
        at = base
        for piece in pieces:
            chunks.append((at, UNIT * piece))
            at += UNIT * piece
    return begins, rhs, chunks, pads, at


def sides(nblock, begins, j):
    left = begins[j] - j * SB
    return left, left + BS * (nblock - 2 * j - 1)


def factor_all(nblock, begins, rhs, packed, factor_ref, z_ref, wh, wl, tiles, y, inv_h, inv_l, hook):
    nsuper = nblock // 2
    spare = nsuper * (nsuper + 1) // 2

    def at(ii):
        return pl.ds(pl.multiple_of(ii * SB, SB), SB)

    def spot(j, ii):
        return (j * (2 * nsuper + 1 - j)) // 2 + ii - j

    def both(j, ii):
        k = spot(j, ii)
        return wh[k], wl[k]

    def fetch(kk):
        if isinstance(kk, int):
            first, second = sides(nblock, begins, kk)
        else:
            first, second = (jnp.int32(v) for v in sides(nblock, begins, 1))
            for j in range(2, nsuper):
                left, right = sides(nblock, begins, j)
                first = jnp.where(kk == j, left, first)
                second = jnp.where(kk == j, right, second)

        @pl.loop(kk, nsuper)
        def _(ii):
            for side, begin in enumerate((first, second)):
                rows = pl.ds(pl.multiple_of(begin + ii * SB, BS), SB)
                tiles[kk % 3, at(ii), side * BS : (side + 1) * BS] = packed[rows, :]

    def fetch_first(low, high):
        @pl.loop(low, high)
        def _(ii):
            for side in range(2):
                rows = pl.ds(pl.multiple_of(2 * SB * ii - BS + side * SB, BS), SB)
                tiles[0, at(ii), side * BS : (side + 1) * BS] = packed[rows, :]

    row = lax.broadcasted_iota(jnp.int32, (BS, BS), 0)
    col = lax.broadcasted_iota(jnp.int32, (BS, BS), 1)
    zero = jnp.zeros((BS, BS), jnp.float32)
    for side in range(3):
        tiles[side, nsuper * SB :, :] = jnp.zeros((SB, SB), jnp.float32)
    y[nsuper] = jnp.zeros((SUB, SB), jnp.float32)
    tiles[0, 0:SB, 0:BS] = packed[0:SB, :]
    tiles[0, 0:SB, BS:SB] = packed[BS : BS + SB, :]
    fetch_first(1, 2)

    def pivot(kk, here, fill):
        diag = tiles[here, at(kk), :]
        la, ea = chol_block(diag[0:BS, 0:BS], fill)
        eas = split(ea)
        l21 = mm3(diag[BS:SB, 0:BS], eas, 1, 1)
        l21s = split(l21)
        lb, eb = chol_block(diag[BS:SB, BS:SB] - mm3(l21s, l21s, 1, 1), fill)
        ec = -mm3(eb, mm3(l21s, eas, 1, 0), 1, 0)
        inv = split(jnp.concatenate(
            [jnp.concatenate([ea, zero], axis=1), jnp.concatenate([ec, eb], axis=1)], axis=0))
        low = jnp.concatenate(
            [jnp.concatenate([la, zero], axis=1), jnp.concatenate([l21, lb], axis=1)], axis=0)
        k = spot(kk, kk)
        wh[k], wl[k] = split(low)
        inv_h[kk], inv_l[kk] = inv
        return inv

    early = iter(range(2 * SUB))
    inv = pivot(0, 0, lambda: hook("pivot%d" % next(early)))
    side = split(mm3(tiles[0, at(1), :], inv, 1, 1))
    wh[1], wl[1] = side
    hook("solved")
    fetch_first(2, nsuper)
    for b in range(nblock):
        y[b // 2, 0:1, (b % 2) * BS : (b % 2 + 1) * BS] = packed[rhs + b : rhs + b + 1, :]
        if b % 2 == 0:
            y[b // 2, 1:SUB, :] = jnp.zeros((SUB - 1, SB), jnp.float32)
    y[0] = mm3(y[0], (inv_h[0], inv_l[0]), 1, 1)
    fetch(1)
    side = both(0, 1)
    tiles[1, at(1), :] = tiles[1, at(1), :] - mm3(side, side, 1, 1)
    fetch(2)

    @pl.loop(1, nsuper)
    def _(kk):
        last = kk - 1
        prev, here, there = (kk + 2) % 3, kk % 3, (kk + 1) % 3
        rest = nsuper - 1 - kk
        final = nsuper - 1
        cursor = [kk + 1, 0]

        def follow(n):
            ii = kk + 1 + n
            valid = ii < nsuper
            value = split(
                mm3(tiles[prev, at(jnp.minimum(ii, final)), :], (inv_h[last], inv_l[last]), 1, 1)
            )
            k = jnp.where(valid, spot(last, ii), spare)
            wh[k], wl[k] = value
            k = jnp.where(valid, ii, nsuper)
            y[k] = y[k] - mm3(y[last], value, 1, 1)

        def update(n):
            first = n < rest
            ii2, j2 = cursor
            valid = first | (ii2 < nsuper)
            j = jnp.where(valid, jnp.where(first, last, j2), 0)
            ii = jnp.where(valid, jnp.where(first, kk + 1 + n, ii2), 0)
            other = jnp.where(valid, jnp.where(first, kk, kk + 1), 0)
            side = jnp.where(valid, jnp.where(first, here, there), 0)
            dest = jnp.where(valid, ii, nsuper)
            moved = jnp.where(first, j2, j2 + 1)
            done = jnp.logical_not(first) & (moved >= kk)
            cursor[0] = jnp.where(done, ii2 + 1, ii2)
            cursor[1] = jnp.where(done, 0, moved)
            tiles[side, at(dest), :] = tiles[side, at(dest), :] - mm3(both(j, ii), both(j, other), 1, 1)

        plan = [[functools.partial(follow, 2 * n), functools.partial(follow, 2 * n + 1)] for n in range(3)]
        plan += [[functools.partial(update, 2 * n), functools.partial(update, 2 * n + 1)] for n in range(3)]
        plan += [[functools.partial(update, n)] for n in range(6, 2 * SUB)]
        steps = iter(plan)

        def fill():
            for f in next(steps):
                f()

        for step in (1, 2):

            @pl.when(kk == step)
            def _():
                hook("first%d" % step)

        ykk = y[kk] - mm3(y[last], both(last, kk), 1, 1)
        inv = pivot(kk, here, fill)
        y[kk] = mm3(ykk, inv, 1, 1)
        value = split(mm3(tiles[here, at(jnp.minimum(kk + 1, final)), :], inv, 1, 1))
        k = jnp.where(kk < final, spot(kk, kk + 1), spare)
        wh[k], wl[k] = value
        dest = jnp.where(kk < final, kk + 1, nsuper)
        tiles[there, at(dest), :] = tiles[there, at(dest), :] - mm3(value, value, 1, 1)

        for step in (1, 2):

            @pl.when(kk == step)
            def _():
                hook("last%d" % step)

        @pl.when(kk + 2 < nsuper)
        def _():
            fetch(kk + 2)

    state = [y[j] for j in range(nsuper)]
    for kk in reversed(range(nsuper)):
        state[kk] = mm3(state[kk], (inv_h[kk], inv_l[kk]), 1, 0)
        x = split(state[kk])
        for j in reversed(range(kk)):
            state[j] = state[j] - mm3(x, both(j, kk), 1, 0)
    for b in range(nblock):
        z_ref[b : b + 1, :] = state[b // 2][0:1, (b % 2) * BS : (b % 2 + 1) * BS]

    per_row, per_col = factor_ref.shape[0], factor_ref.shape[2] // BS
    rows_of, cols_of = nblock // per_row, nblock // per_col
    for r in range(per_row):
        for c in range(per_col):
            rb = r * rows_of + lax.axis_index("gx")
            cb = c * cols_of + lax.axis_index("gy")
            k = spot(cb // 2, jnp.maximum(rb // 2, cb // 2))
            rows = pl.ds(pl.multiple_of((rb % 2) * BS, BS), BS)
            wide = wh[k, rows, :].astype(jnp.float32) + wl[k, rows, :].astype(jnp.float32)
            block = jnp.where(cb % 2 == 0, wide[:, :BS], wide[:, BS:])
            inside = row + rb * BS >= col + cb * BS
            factor_ref[r, :, c * BS : (c + 1) * BS] = jnp.where(inside, block, 0.0)


def make_design(nblock, blocks_ref, coef_ref, design, wide):
    slots, rows = blocks_ref.shape
    chunk = 128

    @pl.loop(0, rows // chunk)
    def _(t):
        at = pl.ds(pl.multiple_of(t * chunk, chunk), chunk)
        idx = blocks_ref[:, at]
        idx = jnp.concatenate([idx] * (SUB // slots), axis=0).T
        labels = [jnp.broadcast_to(idx[:, s : s + 1], (chunk, BS)) for s in range(slots)]
        span = chunk * slots
        wide[...] = coef_ref[pl.ds(pl.multiple_of(t * span, span), span), :].astype(jnp.float32)
        values = [wide[pl.ds(s, chunk, stride=slots), :] for s in range(slots)]
        for b in range(nblock):
            total = jnp.where(labels[0] == b, values[0], 0.0)
            for s in range(1, slots):
                total = jnp.where(labels[s] == b, values[s], total)
            design[at, b * BS : (b + 1) * BS] = total.astype(jnp.bfloat16)


def make_rhs(nblock, scale, base, res_ref, design, term):
    rows = res_ref.shape[1]
    res = res_ref[...]
    high = res.astype(jnp.bfloat16)
    rest = res - high.astype(jnp.float32)
    mid = rest.astype(jnp.bfloat16)
    low = (rest - mid.astype(jnp.float32)).astype(jnp.bfloat16)
    row = lax.broadcasted_iota(jnp.int32, (16, rows), 0)
    parts = jnp.where(
        row == 0,
        high.astype(jnp.float32),
        jnp.where(
            row == 1,
            mid.astype(jnp.float32),
            jnp.where(row == 2, low.astype(jnp.float32), 0.0),
        ),
    ).astype(jnp.bfloat16)
    for b in range(nblock // 2):
        part = mm(parts, design[:, b * SB : (b + 1) * SB], 1, 0, None)
        total = jnp.sum(part, axis=0, keepdims=True) * scale
        term[base + 2 * b : base + 2 * b + 1, :] = total[:, :BS]
        term[base + 2 * b + 1 : base + 2 * b + 2, :] = total[:, BS:]


def gram_panel(nblock, scale, jj, begins, design, term, low, high):
    first, second = sides(nblock, begins, jj)
    right = design[:, jj * SB : (jj + 1) * SB]
    if low == jj:
        begin = begins[jj]
        block = mm(right, right, 0, 0, None) * scale
        term[begin : begin + SB, :] = block[:, :BS]
        begin = SB if jj == 0 else second + jj * SB + BS
        term[begin : begin + BS, :] = block[BS:, BS:]

    @pl.loop(max(low, jj + 1), high)
    def _(ii):
        left = design[:, pl.ds(pl.multiple_of(ii * SB, SB), SB)]
        block = mm(left, design[:, jj * SB : (jj + 1) * SB], 0, 0, None) * scale
        near = 2 * SB * ii - BS if jj == 0 else first + ii * SB
        far = 2 * SB * ii + BS if jj == 0 else second + ii * SB
        term[pl.ds(pl.multiple_of(near, BS), SB), :] = block[:, :BS]
        term[pl.ds(pl.multiple_of(far, BS), SB), :] = block[:, BS:]


def exchanger(chunks, term_ref, out_ref, acc, recv, sends, recvs):
    gx, gy, gz = lax.axis_index("gx"), lax.axis_index("gy"), lax.axis_index("gz")
    x, ylo = gx % 4, gx // 4
    z, core = gy // 2, gy % 2

    def flip(v):
        return v + 1 - 2 * (v % 2)

    def gray(v):
        return (v % 2) + (v // 2) - 2 * (v % 2) * (v // 2)

    y = 2 * gz + ylo
    ynext = 4 * (1 - ylo)
    partner = [
        {"gx": 4 * ylo + flip(x)},
        {"gx": ynext + x},
        {"gy": 2 * flip(z) + core},
        {"gx": 4 * ylo + 3 - x},
        {"gx": ynext + x, "gz": 1 - gz},
        {"gy": 2 * (3 - z) + core},
    ]
    bit = [gray(x), gray(y), gray(z), x // 2, y // 2, z // 2]
    mate = {"gy": 2 * z + 1 - core}
    rows = lambda at, size: pl.ds(pl.multiple_of(at, SUB), size)

    def remote(src, dst, c, s, p, device):
        return pltpu.make_async_remote_copy(
            src_ref=src,
            dst_ref=dst,
            send_sem=sends.at[c, s, p],
            recv_sem=recvs.at[c, s, p],
            device_id=device,
            device_id_type=pl.DeviceIdType.MESH,
        )

    slots, at = {}, 0
    total = sum(size for _, size in chunks) // 2
    for s in range(1, 2 * HALVE + 1):
        slots[s] = at
        at += total >> min(s, HALVE)

    def chunk(c):
        base, size = chunks[c]
        half, part = size // 2, size // 12
        local = [base // 2 + p * part for p in range(6)]
        whole = [base + core * half + p * part for p in range(6)]
        other = [base + (1 - core) * half + p * part for p in range(6)]
        where = []
        for p in range(6):
            steps = [0]
            for level in range(1, HALVE + 1):
                steps.append(steps[-1] + bit[(p + level - 1) % 6] * (part >> level))
            where.append(steps)

        def landing(s, p):
            span = part >> min(s, HALVE)
            slot = slots[s] + ((base // 2) >> min(s, HALVE)) + p * span
            return slice(slot, slot + span)

        def copy(s, p):
            if s == 0:
                src = term_ref.at[rows(other[p], part), :]
                dst = acc.at[local[p] : local[p] + part, :]
                return remote(src, dst, c, 0, p, mate)
            if s <= HALVE:
                span, g = part >> s, (p + s - 1) % 6
                give = where[p][s - 1] + (1 - bit[g]) * span
                src = acc.at[rows(local[p] + give, span), :]
                return remote(src, recv.at[landing(s, p), :], c, s, p, partner[g])
            if s <= 2 * HALVE:
                span, g = part >> HALVE, (p + s - 1) % 6
                src = acc.at[rows(local[p] + where[p][HALVE], span), :]
                return remote(src, recv.at[landing(s, p), :], c, s, p, partner[g])
            level = 3 * HALVE + 1 - s
            block = out_ref.at[rows(whole[p] + where[p][level], part >> level), :]
            device = partner[(p + level - 1) % 6] if level else mate
            return remote(block, block, c, s, p, device)

        def stage(s):
            for p in range(6):
                if s:
                    copy(s - 1, p).wait_recv()
                if s == 1:
                    at = slice(local[p], local[p] + part)
                    acc[at, :] = term_ref[rows(whole[p], part), :] + acc[at, :]
                elif 1 < s <= 2 * HALVE + 1:
                    level = min(s - 1, HALVE)
                    span = part >> level
                    at = rows(local[p] + where[p][level], span)
                    if s - 1 > HALVE:
                        copy(s - 1, p).wait_send()
                    total = acc[at, :] + recv[landing(s - 1, p), :]
                    if s <= 2 * HALVE:
                        acc[at, :] = total
                    else:
                        out_ref[rows(whole[p] + where[p][level], span), :] = total
                if s <= 3 * HALVE + 1:
                    copy(s, p).start()

        def finish():
            for s in range(3 * HALVE + 2):
                if not HALVE < s <= 2 * HALVE:
                    for p in range(6):
                        copy(s, p).wait_send()

        return stage, finish

    runs = [chunk(c) for c in range(len(chunks))]

    def turn(t):
        for (stage, _), rounds in zip(runs, ROUNDS):
            for s, at in enumerate(rounds):
                if at == t:
                    stage(s)

    def finish():
        for _, close in runs:
            close()

    def greet():
        barrier = pltpu.get_barrier_semaphore()
        for device in partner + [mate]:
            pl.semaphore_signal(
                barrier, inc=1, device_id=device, device_id_type=pl.DeviceIdType.MESH
            )

    def meet():
        pl.semaphore_wait(pltpu.get_barrier_semaphore(), len(partner) + 1)

    return turn, finish, greet, meet


ROUNDS = (
    (0, 1, 2, 3, 4, 5, 6, 7, 8, 9, 10, 11),
    (1, 2, 3, 4, 5, 6, 7, 8, 9, 10, 11, 12),
    (2, 3, 4, 5, 6, 7, 8, 9, 10, 11, 12, 13),
    (5, 6, 7, 8, 9, 10, 11, 12, 13, 14, 15, 16),
)
READY = 11
WORK = {0: (0,), 1: (1, 2), 2: (3,), 3: (4,), 4: (5, 6)}
TURNS = {'pivot8': (12,), 'solved': (13,), 'first1': (14,), 'last1': (15, 16)}


def whole_kernel(
    nblock, scale, blocks_ref, coef_ref, res_ref, factor_ref, z_ref,
    design, wide, term, acc, recv, out, wh, wl, tiles, y, inv_h, inv_l, sends, recvs,
):
    nsuper = nblock // 2
    begins, rhs, chunks, pads, _ = layout(nblock)
    turn, finish, greet, meet = exchanger(chunks, term, out, acc, recv, sends, recvs)
    greet()
    for used, end in pads:
        if used < end:
            term[used:end, :] = jnp.zeros((end - used, BS), jnp.float32)

    def gram(j, low=None, high=nsuper):
        gram_panel(nblock, scale, j, begins, design, term, j if low is None else low, high)

    make_design(nblock, blocks_ref, coef_ref, design, wide)
    gram(0, 0, 4)
    meet()
    for t in range(READY + 1):
        turn(t)
        for j in WORK.get(t, ()):
            if j == 0:
                gram(0, 4)
                gram(nsuper - 1)
                make_rhs(nblock, scale, rhs, res_ref, design, term)
            else:
                gram(j)

    def hook(name):
        for t in TURNS.get(name, ()):
            turn(t)

    factor_all(nblock, begins, rhs, out, factor_ref, z_ref, wh, wl, tiles, y, inv_h, inv_l, hook)
    finish()


def on_device(blocks, coefficients, residuals):
    row_count = lax.axis_size("gx")
    col_count = lax.axis_size("gy")
    devices = row_count * col_count * lax.axis_size("gz")
    rows, slots, width = coefficients.shape
    scale = 1.0 / (rows * devices)
    nblock = G // width
    nsuper = nblock // 2
    _, _, chunks, _, total = layout(nblock)
    half = total // 2
    landing = sum(half >> min(s, HALVE) for s in range(1, 2 * HALVE + 1))
    per_row, per_col = nblock // row_count, nblock // col_count
    vmem = pl.BlockSpec(memory_space=pltpu.VMEM)
    sem = pltpu.SemaphoreType.DMA((len(chunks), 3 * HALVE + 2, 6))
    count = nsuper * (nsuper + 1) // 2
    factor, answer = pl.pallas_call(
        functools.partial(whole_kernel, nblock, scale),
        out_shape=(
            jax.ShapeDtypeStruct((per_row, width, per_col * width), jnp.float32),
            jax.ShapeDtypeStruct((nblock, width), jnp.float32),
        ),
        in_specs=[vmem] * 3,
        out_specs=(vmem, vmem),
        scratch_shapes=[
            pltpu.VMEM((rows, G), jnp.bfloat16),
            pltpu.VMEM((BS * slots, width), jnp.float32),
            pltpu.VMEM((total, width), jnp.float32),
            pltpu.VMEM((half, width), jnp.float32),
            pltpu.VMEM((landing, width), jnp.float32),
            pltpu.VMEM((total, width), jnp.float32),
            pltpu.VMEM((count + 1, SB, SB), jnp.bfloat16),
            pltpu.VMEM((count + 1, SB, SB), jnp.bfloat16),
            pltpu.VMEM((3, G + SB, SB), jnp.float32),
            pltpu.VMEM((nsuper + 1, SUB, SB), jnp.float32),
            pltpu.VMEM((nsuper, SB, SB), jnp.bfloat16),
            pltpu.VMEM((nsuper, SB, SB), jnp.bfloat16),
            sem,
            sem,
        ],
        compiler_params=pltpu.CompilerParams(
            vmem_limit_bytes=VMEM_LIMIT, has_side_effects=True, collective_id=0
        ),
    )(blocks.T, coefficients.reshape(rows * slots, width), residuals.reshape(1, rows))
    return (factor.reshape(1, per_row, width, 1, per_col, width), answer)


def solution(mesh):
    in_specs = (
        P(("gx", "gy", "gz"), None),
        P(("gx", "gy", "gz"), None, None),
        P(("gx", "gy", "gz")),
    )
    out_specs = (P("gx", None, None, "gy", None, None), P())
    return jax.shard_map(
        on_device, mesh=mesh, in_specs=in_specs, out_specs=out_specs, check_vma=False
    )
```

time: 152 us -> 143 us (0.941)
  the two profiles are of different devices: /device:TPU:0 before, /device:TPU:1 now
where the time goes in v4:
time: 143 us
  Pallas kernels  140 us (98%)
  local copies, waits for them, and re-layouts  2.39 us (2%)
    pallas_call x1, Pallas kernels, on_device(): pl.pallas_call(functools.partial(whole_kernel, nblock, scale), out_shape=...  140 us

profile of v4, /device:TPU:1, one launch (start us, length us, event | category | flops | bytes accessed | tf_op | source)
XLA Modules:
  0.0 143.1 jit_solution(11779980518776063128)
XLA Ops:
  0.6 140.1 %shard_map.50 = (f32[2,128,256]{2,1,0:T(8,128)}, f32[16,128]{1,0:T(8,128)}) custom-call(s32[4,1024]{1,0:T(4,128)} %bitcast.6, bf16[4096,128]{1,0:T(8,128)(2,1)} %bitcast.4, f32[1,1024]{1,0:T(1,128)} %bitcast.7), custom_call_target="tpu_custom_call" | custom-call | tf_op jit(solution)/shard_map/pallas_call | solution.py:577
  140.7 0.0 copy-start
  140.7 1.8 %reshape.15 = f32[1,2,128,1,2,128]{5,4,2,1,3,0:T(2,128)} reshape(f32[2,128,256]{2,1,0:T(8,128)} %get-tuple-element.4) | data formatting | bytes 524288 | tf_op jit(solution)/shard_map/reshape | solution.py:605
  142.5 0.0 copy-done
  142.5 0.6 copy.7
Async XLA Ops:
  140.7 1.8 %copy-start = (f32[16,128]{1,0:T(8,128)S(1)}, f32[16,128]{1,0:T(8,128)}, u32[]{:S(2)}) copy-start(f32[16,128]{1,0:T(8,128)} %get-tuple-element.11) | copy-start | bytes 24580

commit v5 on v4

--- a/solution.py
+++ b/solution.py
@@ -516,11 +516,11 @@
     (0, 1, 2, 3, 4, 5, 6, 7, 8, 9, 10, 11),
     (1, 2, 3, 4, 5, 6, 7, 8, 9, 10, 11, 12),
     (2, 3, 4, 5, 6, 7, 8, 9, 10, 11, 12, 13),
-    (5, 6, 7, 8, 9, 10, 11, 12, 13, 14, 15, 16),
+    (4, 5, 6, 7, 8, 9, 10, 11, 12, 13, 14, 15),
 )
 READY = 11
-WORK = {0: (0,), 1: (1, 2), 2: (3,), 3: (4,), 4: (5, 6)}
-TURNS = {'pivot8': (12,), 'solved': (13,), 'first1': (14,), 'last1': (15, 16)}
+WORK = {0: (0,), 1: (1, 2), 2: (3,), 3: (4, 5, 6)}
+TURNS = {'pivot8': (12,), 'solved': (13,), 'first1': (14,), 'last1': (15,)}
 
 
 def whole_kernel(

time: 143 us -> 141 us (0.986)
  the two profiles are of different devices: /device:TPU:1 before, /device:TPU:0 now
where the time goes in v5:
time: 141 us
  Pallas kernels  138 us (98%)
  local copies, waits for them, and re-layouts  2.39 us (2%)
    pallas_call x1, Pallas kernels, on_device(): pl.pallas_call(functools.partial(whole_kernel, nblock, scale), out_shape=...  138 us

profile of v5, /device:TPU:0, one launch (start us, length us, event | category | flops | bytes accessed | tf_op | source)
XLA Modules:
  0.0 140.7 jit_solution(10443722751412882340)
XLA Ops:
  0.6 137.6 %shard_map.50 = (f32[2,128,256]{2,1,0:T(8,128)}, f32[16,128]{1,0:T(8,128)}) custom-call(s32[4,1024]{1,0:T(4,128)} %bitcast.6, bf16[4096,128]{1,0:T(8,128)(2,1)} %bitcast.4, f32[1,1024]{1,0:T(1,128)} %bitcast.7), custom_call_target="tpu_custom_call" | custom-call | tf_op jit(solution)/shard_map/pallas_call | solution.py:577
  138.3 0.0 copy-start
  138.3 1.8 %reshape.15 = f32[1,2,128,1,2,128]{5,4,2,1,3,0:T(2,128)} reshape(f32[2,128,256]{2,1,0:T(8,128)} %get-tuple-element.4) | data formatting | bytes 524288 | tf_op jit(solution)/shard_map/reshape | solution.py:605
  140.1 0.0 copy-done
  140.1 0.6 copy.7
Async XLA Ops:
  138.3 1.8 %copy-start = (f32[16,128]{1,0:T(8,128)S(1)}, f32[16,128]{1,0:T(8,128)}, u32[]{:S(2)}) copy-start(f32[16,128]{1,0:T(8,128)} %get-tuple-element.11) | copy-start | bytes 24580
